TPU v7x, 128 devices: a whole 4x4x4 slice. The times are simulated.
128 devices in a mesh: gx: 4 (over x_lo, core), gy: 4 (over y), gz: 8 (over z, x_hi).
Axes of the slice: x: 4 (x_hi: 2, x_lo: 2; x = x_hi * 2 + x_lo), y: 4, z: 4, core: 2. Of those that a mesh axis runs over, the one named last changes fastest.
Arguments:
- orbitals: float32 [64, 32, 32, 1024], P(None, 'gx', 'gy', 'gz'), may hold values from -6 to 6
- potential: float32 [32, 32, 1024], P('gx', 'gy', 'gz'), may hold values from 0 to 0.5
- centre: float32 [64], replicated, may hold values from 3 to 5
- half_width: float32 [64], replicated, may hold values from 3 to 5
Outputs:
- filtered: float32 [64, 32, 32, 1024], P(None, 'gx', 'gy', 'gz')
All inputs are finite; a program needn't handle non-finite values.
Results may differ from a plain program's by a relative error of at most 0.00002.
Values sent between devices are 32-bit elements; how exact they have to be, the bound alone decides.
A program may use at most 64 MiB of HBM per device.

v0:
```python
import jax
import jax.numpy as jnp
from jax import lax
from jax.sharding import PartitionSpec as P

shift_mass = 0.05
jacobi_weight = 2.0 / 3.0


def extended(array, sides, width):
    edges = {}
    for axis, dim in sides:
        size, length = (lax.axis_size(axis), array.shape[dim])
        up = [(i, (i + 1) % size) for i in range(size)]
        last = lax.slice_in_dim(array, length - width, length, axis=dim)
        leading = lax.slice_in_dim(array, 0, width, axis=dim)
        edges[dim] = (
            lax.ppermute(last, axis, up),
            lax.ppermute(leading, axis, [(b, a) for a, b in up]),
        )
    done = []
    for _, dim in sides:
        low, high = edges[dim]
        around = [(width, width) if d in done else (0, 0) for d in range(array.ndim)]
        array = jnp.concatenate([jnp.pad(low, around), array, jnp.pad(high, around)], axis=dim)
        done.append(dim)
    return array


def neighbour_sum(padded):
    total = padded[:, 2:, 1:-1, 1:-1] + padded[:, :-2, 1:-1, 1:-1]
    total = total + padded[:, 1:-1, 2:, 1:-1] + padded[:, 1:-1, :-2, 1:-1]
    return total + padded[:, 1:-1, 1:-1, 2:] + padded[:, 1:-1, 1:-1, :-2]


def restrict(field):
    shape = field.shape
    return 0.5 * field.reshape(shape[0], shape[1] // 2, 2, shape[2] // 2, 2, shape[3] // 2, 2).sum(
        axis=(2, 4, 6)
    )


def average_cells(field):
    shape = field.shape
    return 0.125 * field.reshape(shape[0] // 2, 2, shape[1] // 2, 2, shape[2] // 2, 2).sum(
        axis=(1, 3, 5)
    )


def prolong(field):
    return jnp.repeat(jnp.repeat(jnp.repeat(field, 2, 1), 2, 2), 2, 3)


def relax(level, source, diagonal, coupling, extend):
    applied = diagonal * level - coupling * neighbour_sum(extend(level))
    return level + jacobi_weight * (source - applied) / diagonal


def smooth_two(source, diagonal, extend):
    level = jacobi_weight * source / diagonal
    for sweep_index in range(2):
        level = relax(level, source, diagonal, 0.03125, extend)
    return level


def fine_apply(field, diagonal_fine):
    padded = extended(field, (("gx", 1), ("gy", 2), ("gz", 3)), 1)
    return diagonal_fine * field - 0.5 * neighbour_sum(padded)


def level_one_rim(field):
    return extended(field, (("gx", 1), ("gy", 2), ("gz", 3)), 1)


def level_two_rim(field):
    return extended(field, (("gx", 1), ("gy", 2), ("gz", 3)), 1)


def local(orbitals, potential, centre, half_width):
    middle = centre[:, None, None, None]
    spread = half_width[:, None, None, None]
    diagonal_fine = 3.0 + potential
    first_image = fine_apply(orbitals, diagonal_fine)
    first_order = (first_image - middle * orbitals) / spread
    second_image = fine_apply(first_order, diagonal_fine)
    second_order = 2.0 * (second_image - middle * first_order) / spread - orbitals
    potential_one = average_cells(potential)
    potential_two = average_cells(potential_one)
    diagonal_one = 0.75 + potential_one + shift_mass
    source_one = restrict(second_order)
    level_one = jacobi_weight * source_one / diagonal_one
    level_one = relax(level_one, source_one, diagonal_one, 0.125, level_one_rim)
    residue = source_one - (
        diagonal_one * level_one - 0.125 * neighbour_sum(level_one_rim(level_one))
    )
    source_two = restrict(residue)
    diagonal_two = 0.1875 + potential_two + shift_mass
    level_two = smooth_two(source_two, diagonal_two, level_two_rim)
    level_one = level_one + prolong(level_two)
    level_one = relax(level_one, source_one, diagonal_one, 0.125, level_one_rim)
    return second_order + prolong(level_one)


def solution(mesh):
    in_specs = (P(None, "gx", "gy", "gz"), P("gx", "gy", "gz"), P(), P())
    out_specs = P(None, "gx", "gy", "gz")
    return jax.shard_map(local, mesh=mesh, in_specs=in_specs, out_specs=out_specs, check_vma=False)
```

profile of v0, /device:TPU:1, one launch (start us, length us, event | category | flops | bytes accessed | tf_op | source)
XLA Modules:
  0.0 161.0 jit_solution(2832677705206226167)
XLA Ops:
  0.0 3.9 %copy.5 = f32[64,8,8,128]{0,3,2,1:T(8,128)} copy(f32[64,8,8,128]{3,2,1,0:T(8,128)} %param.4) | data formatting | bytes 4194304 | tf_op args[0]
  6.0 3.6 %collective-permute-start.2 = (f32[64,8,1,128]{0,3,2,1:T(8,128)S(1)}, f32[64,8,1,128]{0,3,2,1:T(8,128)S(1)}, u32[]{:S(2)}, u32[]{:S(2)}) collective-permute-start(f32[64,8,1,128]{0,3,2,1:T(8,128)S(1)} %get-tuple-element.16), channel_id=1, source_target_pairs={{8,0},{16,8},{24,16},{0,24},{9,1},{17,9},{25,17},{1,25},{10,2},{18... | collective-permute-start | bytes 786440 | tf_op jit(solution)/shard_map/ppermute | solution.py:19
  15.0 6.0 %collective-permute-start.4 = (f32[64,8,8,1]{0,3,2,1:T(1,128)S(1)}, f32[64,8,8,1]{0,3,2,1:T(1,128)S(1)}, u32[]{:S(2)}, u32[]{:S(2)}) collective-permute-start(f32[64,8,8,1]{0,3,2,1:T(1,128)S(1)} %get-tuple-element.11), channel_id=1, source_target_pairs={{1,0},{2,1},{3,2},{4,3},{5,4},{6,5},{7,6},{0,7},{9,8},{10,9},{11,1... | collective-permute-start | bytes 49160 | tf_op jit(solution)/shard_map/ppermute | solution.py:19
  29.4 3.9 %collective-permute-done.5 = f32[64,8,8,1]{0,3,2,1:T(1,128)S(1)} collective-permute-done((f32[64,8,8,1]{0,3,2,1:T(1,128)S(1)}, f32[64,8,8,1]{0,3,2,1:T(1,128)S(1)}, u32[]{:S(2)}, u32[]{:S(2)}) %collective-permute-start.5) | collective-permute-done | bytes 16416 | tf_op jit(solution)/shard_map/ppermute | solution.py:18
  33.4 14.0 %fusion.18 = f32[64,8,8,128]{0,3,2,1:T(8,128)S(1)} fusion(f32[64,8,8,1]{0,3,2,1:T(1,128)S(1)} %collective-permute-done.5, f32[64,10,1,128]{0,3,2,1:T(8,128)S(1)} %pad.90, f32[64,10,1,128]{0,3,2,1:T(8,128)S(1)} %pad.91, f32[64,1,8,128]{0,3,2,1:T(8,128)S(1)} %collective-permute-done, f32[64,8,8,128]{0,3,2,1:T(8,128)} %copy.5, ...), kind=kLoop, calls=%fused_computation.37 | loop fusion | flops 18350080 | bytes 5440000 | tf_op jit(solution)/shard_map/div | solution.py:84
  53.1 8.2 %collective-permute-done.8 = f32[64,8,1,128]{0,3,2,1:T(8,128)S(1)} collective-permute-done((f32[64,8,1,128]{0,3,2,1:T(8,128)S(1)}, f32[64,8,1,128]{0,3,2,1:T(8,128)S(1)}, u32[]{:S(2)}, u32[]{:S(2)}) %collective-permute-start.8) | collective-permute-done | bytes 262176 | tf_op jit(solution)/shard_map/ppermute | solution.py:19
  61.4 3.2 %collective-permute-done.9 = f32[64,8,1,128]{0,3,2,1:T(8,128)S(1)} collective-permute-done((f32[64,8,1,128]{0,3,2,1:T(8,128)S(1)}, f32[64,8,1,128]{0,3,2,1:T(8,128)S(1)}, u32[]{:S(2)}, u32[]{:S(2)}) %collective-permute-start.9) | collective-permute-done | bytes 262176 | tf_op jit(solution)/shard_map/ppermute | solution.py:18
  64.7 3.0 %collective-permute-done.11 = f32[64,8,8,1]{0,3,2,1:T(1,128)S(1)} collective-permute-done((f32[64,8,8,1]{0,3,2,1:T(1,128)S(1)}, f32[64,8,8,1]{0,3,2,1:T(1,128)S(1)}, u32[]{:S(2)}, u32[]{:S(2)}) %collective-permute-start.11) | collective-permute-done | bytes 16416 | tf_op jit(solution)/shard_map/ppermute | solution.py:18
  67.7 11.8 %fusion.7 = f32[64,8,8,128]{0,3,2,1:T(8,128)} fusion(f32[64,8,8,128]{0,3,2,1:T(8,128)S(1)} %copy-done, f32[64,8,8,1]{0,3,2,1:T(1,128)S(1)} %collective-permute-done.11, f32[64,10,1,128]{0,3,2,1:T(8,128)S(1)} %pad.94, f32[64,10,1,128]{0,3,2,1:T(8,128)S(1)} %pad.95, f32[64,1,8,128]{0,3,2,1:T(8,128)S(1)} %collective-permute-done.6, ...), kind=kLoop, calls=%fused_computation.8 | loop fusion | flops 19398656 | bytes 7537152 | tf_op jit(solution)/shard_map/sub | solution.py:86
  79.5 4.8 %reduce_sum.36 = f32[64,4,4,64]{0,3,2,1:T(8,128)S(1)} reduce(f32[64,4,2,4,2,64,2]{0,6,5,4,3,2,1:T(2,128)} %bitcast.8, f32[]{:T(128)} %constant.11.clone.1), dimensions={2,4,6}, to_apply=%region_0.1 | reduce | flops 458752 | bytes 2359300 | tf_op jit(solution)/shard_map/reduce_sum | solution.py:38
  84.6 3.5 %collective-permute-start.14 = (f32[64,4,1,64]{0,3,2,1:T(8,128)S(1)}, f32[64,4,1,64]{0,3,2,1:T(8,128)S(1)}, u32[]{:S(2)}, u32[]{:S(2)}) collective-permute-start(f32[64,4,1,64]{0,3,2,1:T(8,128)S(1)} %get-tuple-element.34), channel_id=1, source_target_pairs={{8,0},{16,8},{24,16},{0,24},{9,1},{17,9},{25,17},{1,25},{10,2},{18... | collective-permute-start | bytes 196616 | tf_op jit(solution)/shard_map/ppermute | solution.py:19
  94.7 2.9 %collective-permute-done.17 = f32[64,4,4,1]{0,3,2,1:T(1,128)S(1)} collective-permute-done((f32[64,4,4,1]{0,3,2,1:T(1,128)S(1)}, f32[64,4,4,1]{0,3,2,1:T(1,128)S(1)}, u32[]{:S(2)}, u32[]{:S(2)}) %collective-permute-start.17) | collective-permute-done | bytes 4128 | tf_op jit(solution)/shard_map/ppermute | solution.py:18
  98.1 3.0 %collective-permute-start.20 = (f32[64,4,1,64]{0,3,2,1:T(8,128)S(1)}, f32[64,4,1,64]{0,3,2,1:T(8,128)S(1)}, u32[]{:S(2)}, u32[]{:S(2)}) collective-permute-start(f32[64,4,1,64]{0,3,2,1:T(8,128)S(1)} %get-tuple-element.28), channel_id=1, source_target_pairs={{8,0},{16,8},{24,16},{0,24},{9,1},{17,9},{25,17},{1,25},{10,2},{18... | collective-permute-start | bytes 196616 | tf_op jit(solution)/shard_map/ppermute | solution.py:19
  101.2 3.4 %collective-permute-start.18 = (f32[64,1,4,64]{0,3,2,1:T(8,128)S(1)}, f32[64,1,4,64]{0,3,2,1:T(8,128)S(1)}, u32[]{:S(2)}, u32[]{:S(2)}) collective-permute-start(f32[64,1,4,64]{0,3,2,1:T(8,128)S(1)} %get-tuple-element.26), channel_id=1, source_target_pairs={{32,0},{64,32},{96,64},{0,96},{33,1},{65,33},{97,65},{1,97},{34,2}... | collective-permute-start | bytes 196616 | tf_op jit(solution)/shard_map/ppermute | solution.py:19
  114.9 3.9 %collective-permute-start.24 = (f32[64,1,2,32]{0,3,2,1:T(8,128)S(1)}, f32[64,1,2,32]{0,3,2,1:T(8,128)S(1)}, u32[]{:S(2)}, u32[]{:S(2)}) collective-permute-start(f32[64,1,2,32]{0,3,2,1:T(8,128)S(1)} %get-tuple-element.44), channel_id=1, source_target_pairs={{32,0},{64,32},{96,64},{0,96},{33,1},{65,33},{97,65},{1,97},{34,2}... | collective-permute-start | bytes 49160 | tf_op jit(solution)/shard_map/ppermute | solution.py:19
  122.9 2.7 %collective-permute-done.29 = f32[64,2,2,1]{0,3,2,1:T(1,128)S(1)} collective-permute-done((f32[64,2,2,1]{0,3,2,1:T(1,128)S(1)}, f32[64,2,2,1]{0,3,2,1:T(1,128)S(1)}, u32[]{:S(2)}, u32[]{:S(2)}) %collective-permute-start.29) | collective-permute-done | bytes 1056 | tf_op jit(solution)/shard_map/ppermute | solution.py:18
  125.7 2.7 %collective-permute-start.32 = (f32[64,2,1,32]{0,3,2,1:T(8,128)S(1)}, f32[64,2,1,32]{0,3,2,1:T(8,128)S(1)}, u32[]{:S(2)}, u32[]{:S(2)}) collective-permute-start(f32[64,2,1,32]{0,3,2,1:T(8,128)S(1)} %get-tuple-element.40), channel_id=1, source_target_pairs={{8,0},{16,8},{24,16},{0,24},{9,1},{17,9},{25,17},{1,25},{10,2},{18... | collective-permute-start | bytes 49160 | tf_op jit(solution)/shard_map/ppermute | solution.py:19
  128.5 2.9 %collective-permute-start.30 = (f32[64,1,2,32]{0,3,2,1:T(8,128)S(1)}, f32[64,1,2,32]{0,3,2,1:T(8,128)S(1)}, u32[]{:S(2)}, u32[]{:S(2)}) collective-permute-start(f32[64,1,2,32]{0,3,2,1:T(8,128)S(1)} %get-tuple-element.38), channel_id=1, source_target_pairs={{32,0},{64,32},{96,64},{0,96},{33,1},{65,33},{97,65},{1,97},{34,2}... | collective-permute-start | bytes 49160 | tf_op jit(solution)/shard_map/ppermute | solution.py:19
  131.6 2.9 %collective-permute-start.35 = (f32[64,2,2,1]{0,3,2,1:T(1,128)S(1)}, f32[64,2,2,1]{0,3,2,1:T(1,128)S(1)}, u32[]{:S(2)}, u32[]{:S(2)}) collective-permute-start(f32[64,2,2,1]{0,3,2,1:T(1,128)S(1)} %get-tuple-element.36), channel_id=1, source_target_pairs={{0,1},{1,2},{2,3},{3,4},{4,5},{5,6},{6,7},{7,0},{8,9},{9,10},{10,1... | collective-permute-start | bytes 3080 | tf_op jit(solution)/shard_map/ppermute | solution.py:18
  138.1 3.0 %collective-permute-start.38 = (f32[64,4,1,64]{0,3,2,1:T(8,128)S(1)}, f32[64,4,1,64]{0,3,2,1:T(8,128)S(1)}, u32[]{:S(2)}, u32[]{:S(2)}) collective-permute-start(f32[64,4,1,64]{0,3,2,1:T(8,128)S(1)} %get-tuple-element.22), channel_id=1, source_target_pairs={{8,0},{16,8},{24,16},{0,24},{9,1},{17,9},{25,17},{1,25},{10,2},{18... | collective-permute-start | bytes 196616 | tf_op jit(solution)/shard_map/ppermute | solution.py:19
  141.1 3.1 %collective-permute-start.36 = (f32[64,1,4,64]{0,3,2,1:T(8,128)S(1)}, f32[64,1,4,64]{0,3,2,1:T(8,128)S(1)}, u32[]{:S(2)}, u32[]{:S(2)}) collective-permute-start(f32[64,1,4,64]{0,3,2,1:T(8,128)S(1)} %get-tuple-element.20), channel_id=1, source_target_pairs={{32,0},{64,32},{96,64},{0,96},{33,1},{65,33},{97,65},{1,97},{34,2}... | collective-permute-start | bytes 196616 | tf_op jit(solution)/shard_map/ppermute | solution.py:19
  144.5 2.9 %collective-permute-start.41 = (f32[64,4,4,1]{0,3,2,1:T(1,128)S(1)}, f32[64,4,4,1]{0,3,2,1:T(1,128)S(1)}, u32[]{:S(2)}, u32[]{:S(2)}) collective-permute-start(f32[64,4,4,1]{0,3,2,1:T(1,128)S(1)} %get-tuple-element.18), channel_id=1, source_target_pairs={{0,1},{1,2},{2,3},{3,4},{4,5},{5,6},{6,7},{7,0},{8,9},{9,10},{10,1... | collective-permute-start | bytes 12296 | tf_op jit(solution)/shard_map/ppermute | solution.py:18
  153.7 3.1 %copy_add_fusion = f32[64,8,8,128]{0,3,2,1:T(8,128)} fusion(f32[64,8,8,128]{0,3,2,1:T(8,128)S(1)} %copy-done.1, f32[64,8,8,128]{0,2,3,1:T(8,128)S(1)} %bitcast.9), kind=kLoop, calls=%fused_computation.62 | loop fusion | flops 524288 | bytes 6291456 | tf_op jit(solution)/shard_map/add | solution.py:101
  156.9 4.2 %copy.19 = f32[64,8,8,128]{3,2,1,0:T(8,128)} copy(f32[64,8,8,128]{0,3,2,1:T(8,128)} %copy_add_fusion) | data formatting | bytes 4194304 | tf_op jit(solution)/shard_map/add | solution.py:101
  (136 shorter events, 53.8 us)
Async XLA Ops:
  6.0 15.0 %collective-permute-start.2 = (f32[64,8,1,128]{0,3,2,1:T(8,128)S(1)}, f32[64,8,1,128]{0,3,2,1:T(8,128)S(1)}, u32[]{:S(2)}, u32[]{:S(2)}) collective-permute-start(f32[64,8,1,128]{0,3,2,1:T(8,128)S(1)} %get-tuple-element.16), channel_id=1, source_target_pairs={{8,0},{16,8},{24,16},{0,24},{9,1},{17,9},{25,17},{1,25},{10,2},{18... | collective-permute-start | bytes 786440 | tf_op jit(solution)/shard_map/ppermute | solution.py:19
  9.5 16.8 %collective-permute-start.3 = (f32[64,8,1,128]{0,3,2,1:T(8,128)}, f32[64,8,1,128]{0,3,2,1:T(8,128)}, u32[]{:S(2)}, u32[]{:S(2)}) collective-permute-start(f32[64,8,1,128]{0,3,2,1:T(8,128)} %get-tuple-element.15), channel_id=1, source_target_pairs={{0,8},{8,16},{16,24},{24,0},{1,9},{9,17},{17,25},{25,1},{2,10},{10... | collective-permute-start | bytes 786440 | tf_op jit(solution)/shard_map/ppermute | solution.py:18
  11.8 21.5 %collective-permute-start = (f32[64,1,8,128]{0,3,2,1:T(8,128)}, f32[64,1,8,128]{0,3,2,1:T(8,128)S(1)}, u32[]{:S(2)}, u32[]{:S(2)}) collective-permute-start(f32[64,1,8,128]{0,3,2,1:T(8,128)} %get-tuple-element.14), channel_id=1, source_target_pairs={{32,0},{64,32},{96,64},{0,96},{33,1},{65,33},{97,65},{1,97},{34,2}... | collective-permute-start | bytes 786440 | tf_op jit(solution)/shard_map/ppermute | solution.py:19
  12.8 20.6 %collective-permute-start.1 = (f32[64,1,8,128]{0,3,2,1:T(8,128)}, f32[64,1,8,128]{0,3,2,1:T(8,128)S(1)}, u32[]{:S(2)}, u32[]{:S(2)}) collective-permute-start(f32[64,1,8,128]{0,3,2,1:T(8,128)} %get-tuple-element.13), channel_id=1, source_target_pairs={{0,32},{32,64},{64,96},{96,0},{1,33},{33,65},{65,97},{97,1},{2,34}... | collective-permute-start | bytes 786440 | tf_op jit(solution)/shard_map/ppermute | solution.py:18
  15.0 14.5 %collective-permute-start.4 = (f32[64,8,8,1]{0,3,2,1:T(1,128)S(1)}, f32[64,8,8,1]{0,3,2,1:T(1,128)S(1)}, u32[]{:S(2)}, u32[]{:S(2)}) collective-permute-start(f32[64,8,8,1]{0,3,2,1:T(1,128)S(1)} %get-tuple-element.11), channel_id=1, source_target_pairs={{1,0},{2,1},{3,2},{4,3},{5,4},{6,5},{7,6},{0,7},{9,8},{10,9},{11,1... | collective-permute-start | bytes 49160 | tf_op jit(solution)/shard_map/ppermute | solution.py:19
  21.0 12.4 %collective-permute-start.5 = (f32[64,8,8,1]{0,3,2,1:T(1,128)S(1)}, f32[64,8,8,1]{0,3,2,1:T(1,128)S(1)}, u32[]{:S(2)}, u32[]{:S(2)}) collective-permute-start(f32[64,8,8,1]{0,3,2,1:T(1,128)S(1)} %get-tuple-element.12), channel_id=1, source_target_pairs={{0,1},{1,2},{2,3},{3,4},{4,5},{5,6},{6,7},{7,0},{8,9},{9,10},{10,1... | collective-permute-start | bytes 49160 | tf_op jit(solution)/shard_map/ppermute | solution.py:18
  47.5 13.8 %collective-permute-start.8 = (f32[64,8,1,128]{0,3,2,1:T(8,128)S(1)}, f32[64,8,1,128]{0,3,2,1:T(8,128)S(1)}, u32[]{:S(2)}, u32[]{:S(2)}) collective-permute-start(f32[64,8,1,128]{0,3,2,1:T(8,128)S(1)} %get-tuple-element.10), channel_id=1, source_target_pairs={{8,0},{16,8},{24,16},{0,24},{9,1},{17,9},{25,17},{1,25},{10,2},{18... | collective-permute-start | bytes 786440 | tf_op jit(solution)/shard_map/ppermute | solution.py:19
  50.3 14.3 %collective-permute-start.9 = (f32[64,8,1,128]{0,3,2,1:T(8,128)S(1)}, f32[64,8,1,128]{0,3,2,1:T(8,128)S(1)}, u32[]{:S(2)}, u32[]{:S(2)}) collective-permute-start(f32[64,8,1,128]{0,3,2,1:T(8,128)S(1)} %get-tuple-element.9), channel_id=1, source_target_pairs={{0,8},{8,16},{16,24},{24,0},{1,9},{9,17},{17,25},{25,1},{2,10},{10... | collective-permute-start | bytes 786440 | tf_op jit(solution)/shard_map/ppermute | solution.py:18
  50.3 17.4 %collective-permute-start.6 = (f32[64,1,8,128]{0,3,2,1:T(8,128)S(1)}, f32[64,1,8,128]{0,3,2,1:T(8,128)S(1)}, u32[]{:S(2)}, u32[]{:S(2)}) collective-permute-start(f32[64,1,8,128]{0,3,2,1:T(8,128)S(1)} %get-tuple-element.8), channel_id=1, source_target_pairs={{32,0},{64,32},{96,64},{0,96},{33,1},{65,33},{97,65},{1,97},{34,2}... | collective-permute-start | bytes 786440 | tf_op jit(solution)/shard_map/ppermute | solution.py:19
  50.8 16.9 %collective-permute-start.7 = (f32[64,1,8,128]{0,3,2,1:T(8,128)S(1)}, f32[64,1,8,128]{0,3,2,1:T(8,128)S(1)}, u32[]{:S(2)}, u32[]{:S(2)}) collective-permute-start(f32[64,1,8,128]{0,3,2,1:T(8,128)S(1)} %get-tuple-element.7), channel_id=1, source_target_pairs={{0,32},{32,64},{64,96},{96,0},{1,33},{33,65},{65,97},{97,1},{2,34}... | collective-permute-start | bytes 786440 | tf_op jit(solution)/shard_map/ppermute | solution.py:18
  52.2 12.4 %collective-permute-start.10 = (f32[64,8,8,1]{0,3,2,1:T(1,128)S(1)}, f32[64,8,8,1]{0,3,2,1:T(1,128)S(1)}, u32[]{:S(2)}, u32[]{:S(2)}) collective-permute-start(f32[64,8,8,1]{0,3,2,1:T(1,128)S(1)} %get-tuple-element.5), channel_id=1, source_target_pairs={{1,0},{2,1},{3,2},{4,3},{5,4},{6,5},{7,6},{0,7},{9,8},{10,9},{11,1... | collective-permute-start | bytes 49160 | tf_op jit(solution)/shard_map/ppermute | solution.py:19
  84.6 6.9 %collective-permute-start.14 = (f32[64,4,1,64]{0,3,2,1:T(8,128)S(1)}, f32[64,4,1,64]{0,3,2,1:T(8,128)S(1)}, u32[]{:S(2)}, u32[]{:S(2)}) collective-permute-start(f32[64,4,1,64]{0,3,2,1:T(8,128)S(1)} %get-tuple-element.34), channel_id=1, source_target_pairs={{8,0},{16,8},{24,16},{0,24},{9,1},{17,9},{25,17},{1,25},{10,2},{18... | collective-permute-start | bytes 196616 | tf_op jit(solution)/shard_map/ppermute | solution.py:19
  88.1 9.6 %collective-permute-start.12 = (f32[64,1,4,64]{0,3,2,1:T(8,128)S(1)}, f32[64,1,4,64]{0,3,2,1:T(8,128)S(1)}, u32[]{:S(2)}, u32[]{:S(2)}) collective-permute-start(f32[64,1,4,64]{0,3,2,1:T(8,128)S(1)} %get-tuple-element.32), channel_id=1, source_target_pairs={{32,0},{64,32},{96,64},{0,96},{33,1},{65,33},{97,65},{1,97},{34,2}... | collective-permute-start | bytes 196616 | tf_op jit(solution)/shard_map/ppermute | solution.py:19
  90.5 7.1 %collective-permute-start.13 = (f32[64,1,4,64]{0,3,2,1:T(8,128)S(1)}, f32[64,1,4,64]{0,3,2,1:T(8,128)S(1)}, u32[]{:S(2)}, u32[]{:S(2)}) collective-permute-start(f32[64,1,4,64]{0,3,2,1:T(8,128)S(1)} %get-tuple-element.31), channel_id=1, source_target_pairs={{0,32},{32,64},{64,96},{96,0},{1,33},{33,65},{65,97},{97,1},{2,34}... | collective-permute-start | bytes 196616 | tf_op jit(solution)/shard_map/ppermute | solution.py:18
  98.1 7.2 %collective-permute-start.20 = (f32[64,4,1,64]{0,3,2,1:T(8,128)S(1)}, f32[64,4,1,64]{0,3,2,1:T(8,128)S(1)}, u32[]{:S(2)}, u32[]{:S(2)}) collective-permute-start(f32[64,4,1,64]{0,3,2,1:T(8,128)S(1)} %get-tuple-element.28), channel_id=1, source_target_pairs={{8,0},{16,8},{24,16},{0,24},{9,1},{17,9},{25,17},{1,25},{10,2},{18... | collective-permute-start | bytes 196616 | tf_op jit(solution)/shard_map/ppermute | solution.py:19
  101.1 6.7 %collective-permute-start.21 = (f32[64,4,1,64]{0,3,2,1:T(8,128)S(1)}, f32[64,4,1,64]{0,3,2,1:T(8,128)S(1)}, u32[]{:S(2)}, u32[]{:S(2)}) collective-permute-start(f32[64,4,1,64]{0,3,2,1:T(8,128)S(1)} %get-tuple-element.27), channel_id=1, source_target_pairs={{0,8},{8,16},{16,24},{24,0},{1,9},{9,17},{17,25},{25,1},{2,10},{10... | collective-permute-start | bytes 196616 | tf_op jit(solution)/shard_map/ppermute | solution.py:18
  101.2 10.2 %collective-permute-start.18 = (f32[64,1,4,64]{0,3,2,1:T(8,128)S(1)}, f32[64,1,4,64]{0,3,2,1:T(8,128)S(1)}, u32[]{:S(2)}, u32[]{:S(2)}) collective-permute-start(f32[64,1,4,64]{0,3,2,1:T(8,128)S(1)} %get-tuple-element.26), channel_id=1, source_target_pairs={{32,0},{64,32},{96,64},{0,96},{33,1},{65,33},{97,65},{1,97},{34,2}... | collective-permute-start | bytes 196616 | tf_op jit(solution)/shard_map/ppermute | solution.py:19
  104.6 6.8 %collective-permute-start.19 = (f32[64,1,4,64]{0,3,2,1:T(8,128)S(1)}, f32[64,1,4,64]{0,3,2,1:T(8,128)S(1)}, u32[]{:S(2)}, u32[]{:S(2)}) collective-permute-start(f32[64,1,4,64]{0,3,2,1:T(8,128)S(1)} %get-tuple-element.25), channel_id=1, source_target_pairs={{0,32},{32,64},{64,96},{96,0},{1,33},{33,65},{65,97},{97,1},{2,34}... | collective-permute-start | bytes 196616 | tf_op jit(solution)/shard_map/ppermute | solution.py:18
  112.2 7.3 %collective-permute-start.26 = (f32[64,2,1,32]{0,3,2,1:T(8,128)S(1)}, f32[64,2,1,32]{0,3,2,1:T(8,128)S(1)}, u32[]{:S(2)}, u32[]{:S(2)}) collective-permute-start(f32[64,2,1,32]{0,3,2,1:T(8,128)S(1)} %get-tuple-element.46), channel_id=1, source_target_pairs={{8,0},{16,8},{24,16},{0,24},{9,1},{17,9},{25,17},{1,25},{10,2},{18... | collective-permute-start | bytes 49160 | tf_op jit(solution)/shard_map/ppermute | solution.py:19
  114.9 7.0 %collective-permute-start.27 = (f32[64,2,1,32]{0,3,2,1:T(8,128)S(1)}, f32[64,2,1,32]{0,3,2,1:T(8,128)S(1)}, u32[]{:S(2)}, u32[]{:S(2)}) collective-permute-start(f32[64,2,1,32]{0,3,2,1:T(8,128)S(1)} %get-tuple-element.45), channel_id=1, source_target_pairs={{0,8},{8,16},{16,24},{24,0},{1,9},{9,17},{17,25},{25,1},{2,10},{10... | collective-permute-start | bytes 49160 | tf_op jit(solution)/shard_map/ppermute | solution.py:18
  114.9 10.7 %collective-permute-start.24 = (f32[64,1,2,32]{0,3,2,1:T(8,128)S(1)}, f32[64,1,2,32]{0,3,2,1:T(8,128)S(1)}, u32[]{:S(2)}, u32[]{:S(2)}) collective-permute-start(f32[64,1,2,32]{0,3,2,1:T(8,128)S(1)} %get-tuple-element.44), channel_id=1, source_target_pairs={{32,0},{64,32},{96,64},{0,96},{33,1},{65,33},{97,65},{1,97},{34,2}... | collective-permute-start | bytes 49160 | tf_op jit(solution)/shard_map/ppermute | solution.py:19
  118.8 6.8 %collective-permute-start.25 = (f32[64,1,2,32]{0,3,2,1:T(8,128)S(1)}, f32[64,1,2,32]{0,3,2,1:T(8,128)S(1)}, u32[]{:S(2)}, u32[]{:S(2)}) collective-permute-start(f32[64,1,2,32]{0,3,2,1:T(8,128)S(1)} %get-tuple-element.43), channel_id=1, source_target_pairs={{0,32},{32,64},{64,96},{96,0},{1,33},{33,65},{65,97},{97,1},{2,34}... | collective-permute-start | bytes 49160 | tf_op jit(solution)/shard_map/ppermute | solution.py:18
  128.5 9.1 %collective-permute-start.30 = (f32[64,1,2,32]{0,3,2,1:T(8,128)S(1)}, f32[64,1,2,32]{0,3,2,1:T(8,128)S(1)}, u32[]{:S(2)}, u32[]{:S(2)}) collective-permute-start(f32[64,1,2,32]{0,3,2,1:T(8,128)S(1)} %get-tuple-element.38), channel_id=1, source_target_pairs={{32,0},{64,32},{96,64},{0,96},{33,1},{65,33},{97,65},{1,97},{34,2}... | collective-permute-start | bytes 49160 | tf_op jit(solution)/shard_map/ppermute | solution.py:19
  141.1 9.5 %collective-permute-start.36 = (f32[64,1,4,64]{0,3,2,1:T(8,128)S(1)}, f32[64,1,4,64]{0,3,2,1:T(8,128)S(1)}, u32[]{:S(2)}, u32[]{:S(2)}) collective-permute-start(f32[64,1,4,64]{0,3,2,1:T(8,128)S(1)} %get-tuple-element.20), channel_id=1, source_target_pairs={{32,0},{64,32},{96,64},{0,96},{33,1},{65,33},{97,65},{1,97},{34,2}... | collective-permute-start | bytes 196616 | tf_op jit(solution)/shard_map/ppermute | solution.py:19
  (24 other events, 195.1 us)
where the time goes:
time: 164 us; the launch traced here: 161 us
  starting transfers between devices  65.4 us (40%)
  waiting for transfers between devices  37.5 us (23%)
  other arithmetic  36.1 us (22%)
  local copies, waits for them, and re-layouts  21.5 us (13%)
    ppermute x21, starting transfers between devices, extended(): lax.ppermute(leading, axis, [(b, a) for a, b in up])  47.4 us
    ppermute x21, waiting for transfers between devices, extended(): lax.ppermute(last, axis, up)  22.8 us
    ppermute x21, starting transfers between devices, extended(): lax.ppermute(last, axis, up)  18.1 us
    ppermute x21, waiting for transfers between devices, extended(): lax.ppermute(leading, axis, [(b, a) for a, b in up])  14.7 us
    div x1, other arithmetic, local(): first_order = (first_image - middle * orbitals) / spread  14 us
    sub x1, other arithmetic, local(): 2.0 * (second_image - middle * first_order) / spread - orbitals  11.8 us
    reduce_sum x2, other arithmetic, restrict(): field.reshape(shape[0], shape[1] // 2, 2, shape[2] // 2, 2, shape[3] // 2...  5.15 us
    unnamed x13, local copies, waits for them, and re-layouts  5.06 us
  transfers between devices with their start and end apart: 42, of which 15 were waited for; matrix products, arithmetic and copies ran while one was open for 5% of the time, Pallas kernels for 0%

commit v1 on v0

v1 whole, which is shorter than its diff:
```python
import jax
import jax.numpy as jnp
from jax import lax
from jax.experimental import pallas as pl
from jax.experimental.pallas import tpu as pltpu
from jax.sharding import PartitionSpec as P

MESH = pl.DeviceIdType.MESH
shift_mass = 0.05
jacobi_weight = 2.0 / 3.0
SUB, LANES = 8, 128
AXES = ("gx", "gy", "gz")
SIDES = (("gx", 1), ("gx", -1), ("gy", 1), ("gy", -1), ("gz", 1), ("gz", -1))


def lane():
    return lax.broadcasted_iota(jnp.int32, (SUB, LANES), 1)


def sublane():
    return lax.broadcasted_iota(jnp.int32, (SUB, LANES), 0)


def roll(value, shift):
    shift = shift % LANES
    return value if shift == 0 else pltpu.roll(value, shift, 1)


def turn(rows):
    at, rows = sublane(), list(rows)
    for d in (4, 2, 1):
        low = (at & d) == 0
        for i in range(SUB):
            if i & d == 0:
                a, b = rows[i], rows[i + d]
                rows[i] = jnp.where(low, a, pltpu.roll(b, d, 0))
                rows[i + d] = jnp.where(low, pltpu.roll(a, SUB - d, 0), b)
    return rows


def packed(total, value, start, width):
    at = lane()
    moved = roll(value, start + width // 2)
    if total is None:
        return moved
    return jnp.where((at >= start) & (at < start + width), moved, total)


def along_z(value, rims, start, width):
    at, half = lane(), width // 2
    outer = roll(rims, -(start + half))
    left = jnp.where(at < half, outer, roll(value, half))
    right = jnp.where(at >= LANES - half, outer, roll(value, -half))
    return left + right


def met(from_left, from_right, width):
    half = width // 2
    return jnp.where((lane() & half) != 0, roll(from_left, half), roll(from_right, -half))


def pair_sum(value, cell):
    at = lane()
    return value + jnp.where((at & cell) == 0, roll(value, -cell), roll(value, cell))


def kernel(bands, nx, ny, chunks, orb_hbm, pot_ref, mid_ref, half_ref, out_ref,
           stage, A, F, S2, DG, D1, W1, W2, D2, MID, INV, FZS, FZR,
           B1, U1a, U1b, U1c, V1, U2a, U2b, B2, X1S, X1R, Z1S, Z1R, X2S, X2R, Z2S, Z2R,
           in_sem, out_sem, fs, fr, as_, ar, bs, br):
    deep = bands // chunks
    inner = deep // SUB
    groups = bands // SUB
    cx, cy = nx // 2, ny // 2
    ex, ey = nx // 4, ny // 4
    peers = []
    for axis, step in SIDES:
        n = lax.axis_size(axis)
        peers.append({axis: lax.rem(lax.axis_index(axis) + (n + step), n)})

    def load(c):
        part = pl.ds(c * deep, deep)
        return pltpu.make_async_copy(orb_hbm.at[part], stage.at[part], in_sem.at[c])

    for c in range(chunks):
        load(c).start()
    barrier = pltpu.get_barrier_semaphore()
    for peer in peers:
        pl.semaphore_signal(barrier, inc=1, device_id=peer, device_id_type=MESH)

    def shape(value):
        return jnp.broadcast_to(value, (SUB, LANES))

    at = sublane()
    for g in range(groups):
        mid = jnp.full((SUB, LANES), mid_ref[g * SUB], jnp.float32)
        half = jnp.full((SUB, LANES), half_ref[g * SUB], jnp.float32)
        for s in range(1, SUB):
            mid = jnp.where(at == s, mid_ref[g * SUB + s], mid)
            half = jnp.where(at == s, half_ref[g * SUB + s], half)
        MID[g] = 3.0 - mid
        INV[g] = 1.0 / half
    ones = {}
    for X in range(cx):
        for Y in range(cy):
            total = None
            for dx in range(2):
                for dy in range(2):
                    k = (2 * X + dx) * ny + 2 * Y + dy
                    row = shape(pot_ref[pl.ds(k, 1), :])
                    DG[k] = row
                    total = row if total is None else total + row
            one = 0.125 * pair_sum(total, 1)
            ones[X, Y] = one
            diagonal = 0.75 + one + shift_mass
            D1[X * cy + Y] = diagonal
            W1[X * cy + Y] = jacobi_weight / diagonal
    for X in range(ex):
        for Y in range(ey):
            total = (ones[2 * X, 2 * Y] + ones[2 * X + 1, 2 * Y]) + (ones[2 * X, 2 * Y + 1] + ones[2 * X + 1, 2 * Y + 1])
            diagonal = 0.1875 + 0.125 * pair_sum(total, 2) + shift_mass
            D2[X * ey + Y] = diagonal
            W2[X * ey + Y] = jacobi_weight / diagonal

    def send(src, dst, s, r, d):
        return pltpu.make_async_remote_copy(
            src_ref=src, dst_ref=dst, send_sem=s, recv_sem=r, device_id=peers[d], device_id_type=MESH)

    def fine(buffer, rnd, c):
        ends = (
            (buffer.at[c, nx, pl.ds(1, ny)], buffer.at[c, 0, pl.ds(1, ny)]),
            (buffer.at[c, 1, pl.ds(1, ny)], buffer.at[c, nx + 1, pl.ds(1, ny)]),
            (buffer.at[c, pl.ds(1, nx), ny], buffer.at[c, pl.ds(1, nx), 0]),
            (buffer.at[c, pl.ds(1, nx), 1], buffer.at[c, pl.ds(1, nx), ny + 1]),
            (FZS.at[rnd, 0, c], FZR.at[rnd, 0, c]),
            (FZS.at[rnd, 1, c], FZR.at[rnd, 1, c]),
        )
        return [send(a, b, fs.at[rnd, c, d], fr.at[rnd, c, d], d) for d, (a, b) in enumerate(ends)]

    def fine_edges(rnd, c, totals):
        odd = (lane() & 1) != 0
        for i in range(inner // 2):
            a, b = totals[2 * i], totals[2 * i + 1]
            FZS[rnd, 0, c, i] = jnp.where(odd, roll(a, 1), b)
            FZS[rnd, 1, c, i] = jnp.where(odd, b, roll(a, -1))

    def fine_rims(rnd, c):
        odd = (lane() & 1) != 0
        rims = []
        for i in range(inner // 2):
            low, high = FZR[rnd, 0, c, i], FZR[rnd, 1, c, i]
            rims.append(jnp.where(odd, low, high))
            rims.append(jnp.where(odd, roll(low, 1), roll(high, -1)))
        return rims

    def start_fine(c):
        load(c).wait()
        totals = [None] * inner
        for j in range(inner):
            for x in range(nx):
                rows = turn([stage[c * deep + j * SUB + i, x * ny:(x + 1) * ny, :] for i in range(SUB)])
                for y in range(ny):
                    A[c, x + 1, y + 1, j * SUB:(j + 1) * SUB, :] = rows[y]
                    totals[j] = packed(totals[j], rows[y], 2 * (x * ny + y), 2)
        fine_edges(0, c, totals)

    def apply(buffer, c, x, y, j, rims):
        band = slice(j * SUB, (j + 1) * SUB)
        v = buffer[c, x + 1, y + 1, band, :]
        total = buffer[c, x, y + 1, band, :] + buffer[c, x + 2, y + 1, band, :]
        total = total + buffer[c, x + 1, y, band, :] + buffer[c, x + 1, y + 2, band, :]
        total = total + along_z(v, rims[j], 2 * (x * ny + y), 2)
        return v, (DG[x * ny + y] + MID[c * inner + j]) * v - 0.5 * total

    def first_pass(c):
        rims, totals = fine_rims(0, c), [None] * inner
        for j in range(inner):
            inv = INV[c * inner + j]
            for x in range(nx):
                for y in range(ny):
                    _, image = apply(A, c, x, y, j, rims)
                    value = image * inv
                    F[c, x + 1, y + 1, j * SUB:(j + 1) * SUB, :] = value
                    totals[j] = packed(totals[j], value, 2 * (x * ny + y), 2)
        fine_edges(1, c, totals)

    def faces(buffer, n, m, tile, count):
        even = (lane() & 1) == 0
        rows = pl.ds(tile, SUB)
        lines = ([(n, y) for y in range(1, m + 1)], [(1, y) for y in range(1, m + 1)],
                 [(x, m) for x in range(1, n + 1)], [(x, 1) for x in range(1, n + 1)])
        return [[jnp.where(even, buffer[l[2 * p][0], l[2 * p][1], rows, :], buffer[l[2 * p + 1][0], l[2 * p + 1][1], rows, :])
                 for p in range(count)] for l in lines]

    def unfaces(buffer, received, rnd, n, m, count, g):
        even = (lane() & 1) == 0
        rows = slice(g * SUB, (g + 1) * SUB)
        lines = ([(0, y) for y in range(1, m + 1)], [(n + 1, y) for y in range(1, m + 1)],
                 [(x, 0) for x in range(1, n + 1)], [(x, m + 1) for x in range(1, n + 1)])
        for d, l in enumerate(lines):
            for p in range(count):
                both = received[rnd, d, p, rows, :]
                buffer[l[2 * p][0], l[2 * p][1], rows, :] = jnp.where(even, both, roll(both, 1))
                buffer[l[2 * p + 1][0], l[2 * p + 1][1], rows, :] = jnp.where(even, roll(both, -1), both)

    def second_pass(c):
        rims = fine_rims(1, c)
        zs = None
        for j in range(inner):
            band = slice(j * SUB, (j + 1) * SUB)
            rows = pl.ds(c * deep + j * SUB, SUB)
            scale = 2.0 * INV[c * inner + j]
            for X in range(cx):
                for Y in range(cy):
                    total = None
                    for dx in range(2):
                        for dy in range(2):
                            x, y = 2 * X + dx, 2 * Y + dy
                            _, image = apply(F, c, x, y, j, rims)
                            value = image * scale - A[c, x + 1, y + 1, band, :]
                            S2[c, x, y, band, :] = value
                            total = value if total is None else total + value
                    source = 0.5 * pair_sum(total, 1)
                    B1[X * cy + Y, rows, :] = source
                    level = W1[X * cy + Y] * source
                    U1a[X + 1, Y + 1, rows, :] = level
                    zs = packed(zs, level, j * 64 + 4 * (X * cy + Y), 4)
            for d, line in enumerate(faces(U1a, cx, cy, c * deep + j * SUB, cy // 2)):
                for p, value in enumerate(line):
                    X1S[0, d, p, rows, :] = value
        Z1S[0, c] = zs

    def one_chunk(c):
        rows = pl.ds(c * deep, deep)
        copies = [send(X1S.at[0, d, :, rows], X1R.at[0, d, :, rows], as_.at[c, d], ar.at[c, d], d) for d in range(4)]
        return copies + [send(Z1S.at[0, c], Z1R.at[0, d - 4, c], as_.at[c, d], ar.at[c, d], d) for d in (4, 5)]

    def one(rnd):
        k = rnd - 1
        copies = [send(X1S.at[rnd, d], X1R.at[rnd, d], bs.at[k, d], br.at[k, d], d) for d in range(4)]
        return copies + [send(Z1S.at[rnd], Z1R.at[rnd, d - 4], bs.at[k, d], br.at[k, d], d) for d in (4, 5)]

    def two(rnd):
        k = 2 + rnd
        copies = [send(X2S.at[rnd, d], X2R.at[rnd, d], bs.at[k, d], br.at[k, d], d) for d in range(4)]
        return copies + [send(Z2S.at[rnd], Z2R.at[rnd, d - 4], bs.at[k, d], br.at[k, d], d) for d in (4, 5)]

    def around(buffer, X, Y, g, rims, start, width):
        rows = slice(g * SUB, (g + 1) * SUB)
        u = buffer[X + 1, Y + 1, rows, :]
        total = buffer[X, Y + 1, rows, :] + buffer[X + 2, Y + 1, rows, :]
        total = total + buffer[X + 1, Y, rows, :] + buffer[X + 1, Y + 2, rows, :]
        return u, total + along_z(u, rims, start, width)

    def send_faces(buffer, out, rnd, n, m, g):
        rows = slice(g * SUB, (g + 1) * SUB)
        for d, line in enumerate(faces(buffer, n, m, g * SUB, m // 2)):
            for p, value in enumerate(line):
                out[rnd, d, p, rows, :] = value

    def start1(g, X, Y):
        return (g % 2) * 64 + 4 * (X * cy + Y)

    def start2(g, X, Y):
        return (g % 4) * 32 + 8 * (X * ey + Y)

    def sweep_one(buffer, rnd, g, rims, put):
        rows = slice(g * SUB, (g + 1) * SUB)
        for X in range(cx):
            for Y in range(cy):
                u, total = around(buffer, X, Y, g, rims, start1(g, X, Y), 4)
                source = B1[X * cy + Y, rows, :]
                put(X, Y, u * (1.0 - jacobi_weight) + W1[X * cy + Y] * (source + 0.125 * total))

    pl.semaphore_wait(barrier, 6)

    @pl.loop(0, chunks)
    def _(c):
        start_fine(c)
        for copy in fine(A, 0, c):
            copy.start()

    @pl.loop(0, chunks)
    def _(c):
        for copy in fine(A, 0, c):
            copy.wait_recv()
        first_pass(c)
        for copy in fine(F, 1, c):
            copy.start()

    @pl.loop(0, chunks)
    def _(c):
        for copy in fine(F, 1, c):
            copy.wait_recv()
        second_pass(c)
        for copy in one_chunk(c):
            copy.start()

    for c in range(chunks):
        for copy in one_chunk(c):
            copy.wait_recv()
    zs = None
    for g in range(groups):
        rows = slice(g * SUB, (g + 1) * SUB)
        unfaces(U1a, X1R, 0, cx, cy, cy // 2, g)
        rims = met(Z1R[0, 0, g // 2], Z1R[0, 1, g // 2], 4)
        zs = None if g % 2 == 0 else zs
        for X in range(cx):
            for Y in range(cy):
                u, total = around(U1a, X, Y, g, rims, start1(g, X, Y), 4)
                value = u * (1.0 - jacobi_weight) + W1[X * cy + Y] * (B1[X * cy + Y, rows, :] + 0.125 * total)
                U1b[X + 1, Y + 1, rows, :] = value
                zs = packed(zs, value, start1(g, X, Y), 4)
        send_faces(U1b, X1S, 1, cx, cy, g)
        if g % 2 == 1:
            Z1S[1, g // 2] = zs
    for copy in one(1):
        copy.start()
    for copy in one(1):
        copy.wait_recv()
    for g in range(groups):
        rows = slice(g * SUB, (g + 1) * SUB)
        unfaces(U1b, X1R, 1, cx, cy, cy // 2, g)
        rims = met(Z1R[1, 0, g // 2], Z1R[1, 1, g // 2], 4)
        zs = None if g % 4 == 0 else zs
        for X in range(ex):
            for Y in range(ey):
                sums = None
                for dx in range(2):
                    for dy in range(2):
                        x, y = 2 * X + dx, 2 * Y + dy
                        u, total = around(U1b, x, y, g, rims, start1(g, x, y), 4)
                        residue = B1[x * cy + y, rows, :] - D1[x * cy + y] * u + 0.125 * total
                        sums = residue if sums is None else sums + residue
                source = 0.5 * pair_sum(sums, 2)
                B2[X * ey + Y, rows, :] = source
                level = W2[X * ey + Y] * source
                U2a[X + 1, Y + 1, rows, :] = level
                zs = packed(zs, level, start2(g, X, Y), 8)
        send_faces(U2a, X2S, 0, ex, ey, g)
        if g % 4 == 3:
            Z2S[0, g // 4] = zs
    for copy in two(0):
        copy.start()
    for copy in two(0):
        copy.wait_recv()
    for g in range(groups):
        rows = slice(g * SUB, (g + 1) * SUB)
        unfaces(U2a, X2R, 0, ex, ey, ey // 2, g)
        rims = met(Z2R[0, 0, g // 4], Z2R[0, 1, g // 4], 8)
        zs = None if g % 4 == 0 else zs
        for X in range(ex):
            for Y in range(ey):
                u, total = around(U2a, X, Y, g, rims, start2(g, X, Y), 8)
                value = u * (1.0 - jacobi_weight) + W2[X * ey + Y] * (B2[X * ey + Y, rows, :] + 0.03125 * total)
                U2b[X + 1, Y + 1, rows, :] = value
                zs = packed(zs, value, start2(g, X, Y), 8)
        send_faces(U2b, X2S, 1, ex, ey, g)
        if g % 4 == 3:
            Z2S[1, g // 4] = zs
    for copy in two(1):
        copy.start()
    for copy in two(1):
        copy.wait_recv()
    for g in range(groups):
        rows = slice(g * SUB, (g + 1) * SUB)
        unfaces(U2b, X2R, 1, ex, ey, ey // 2, g)
        rims = met(Z2R[1, 0, g // 4], Z2R[1, 1, g // 4], 8)
        zs = None if g % 2 == 0 else zs
        for X in range(ex):
            for Y in range(ey):
                u, total = around(U2b, X, Y, g, rims, start2(g, X, Y), 8)
                value = u * (1.0 - jacobi_weight) + W2[X * ey + Y] * (B2[X * ey + Y, rows, :] + 0.03125 * total)
                for dx in range(2):
                    for dy in range(2):
                        x, y = 2 * X + dx, 2 * Y + dy
                        level = U1b[x + 1, y + 1, rows, :] + value
                        U1c[x + 1, y + 1, rows, :] = level
                        zs = packed(zs, level, start1(g, x, y), 4)
        send_faces(U1c, X1S, 2, cx, cy, g)
        if g % 2 == 1:
            Z1S[2, g // 2] = zs
    for copy in one(2):
        copy.start()
    for copy in one(2):
        copy.wait_recv()
    for g in range(groups):
        rows = slice(g * SUB, (g + 1) * SUB)
        unfaces(U1c, X1R, 2, cx, cy, cy // 2, g)
        rims = met(Z1R[2, 0, g // 2], Z1R[2, 1, g // 2], 4)

        def keep(X, Y, value, rows=rows):
            V1[X * cy + Y, rows, :] = value

        sweep_one(U1c, 2, g, rims, keep)

    def store(c):
        part = pl.ds(c * deep, deep)
        return pltpu.make_async_copy(stage.at[part], out_ref.at[part], out_sem.at[c])

    @pl.loop(0, chunks)
    def _(c):
        for j in range(inner):
            rows = pl.ds(c * deep + j * SUB, SUB)
            for x in range(nx):
                values = turn([S2[c, x, y, j * SUB:(j + 1) * SUB, :] + V1[(x // 2) * cy + y // 2, rows, :] for y in range(ny)])
                for i in range(SUB):
                    stage[c * deep + j * SUB + i, x * ny:(x + 1) * ny, :] = values[i]
        store(c).start()

    for c in range(chunks):
        for copy in fine(A, 0, c) + fine(F, 1, c) + one_chunk(c):
            copy.wait_send()
        store(c).wait()
    for copy in one(1) + one(2) + two(0) + two(1):
        copy.wait_send()


def local(orbitals, potential, centre, half_width):
    bands, nx, ny, nz = orbitals.shape
    chunks = 4
    deep = bands // chunks
    cx, cy, ex, ey = nx // 2, ny // 2, nx // 4, ny // 4
    groups = bands // SUB
    vmem = lambda *s: pltpu.VMEM(s, jnp.float32)
    dma = lambda *s: pltpu.SemaphoreType.DMA(s)
    import functools

    out = pl.pallas_call(
        functools.partial(kernel, bands, nx, ny, chunks),
        name="filter_orbitals",
        out_shape=jax.ShapeDtypeStruct((bands, nx * ny, nz), jnp.float32),
        in_specs=[pl.BlockSpec(memory_space=pl.ANY), pl.BlockSpec(memory_space=pltpu.VMEM),
                  pl.BlockSpec(memory_space=pltpu.SMEM), pl.BlockSpec(memory_space=pltpu.SMEM)],
        out_specs=pl.BlockSpec(memory_space=pl.ANY),
        scratch_shapes=[
            vmem(bands, nx * ny, nz),
            vmem(chunks, nx + 2, ny + 2, deep, nz), vmem(chunks, nx + 2, ny + 2, deep, nz), vmem(chunks, nx, ny, deep, nz),
            vmem(nx * ny, SUB, nz), vmem(cx * cy, SUB, nz), vmem(cx * cy, SUB, nz), vmem(ex * ey, SUB, nz), vmem(ex * ey, SUB, nz),
            vmem(groups, SUB, nz), vmem(groups, SUB, nz),
            vmem(2, 2, chunks, deep // 16, SUB, nz), vmem(2, 2, chunks, deep // 16, SUB, nz),
            vmem(cx * cy, bands, nz),
            vmem(cx + 2, cy + 2, bands, nz), vmem(cx + 2, cy + 2, bands, nz), vmem(cx + 2, cy + 2, bands, nz),
            vmem(cx * cy, bands, nz),
            vmem(ex + 2, ey + 2, bands, nz), vmem(ex + 2, ey + 2, bands, nz), vmem(ex * ey, bands, nz),
            vmem(3, 4, cy // 2, bands, nz), vmem(3, 4, cy // 2, bands, nz),
            vmem(3, groups // 2, SUB, nz), vmem(3, 2, groups // 2, SUB, nz),
            vmem(2, 4, ey // 2, bands, nz), vmem(2, 4, ey // 2, bands, nz),
            vmem(2, groups // 4, SUB, nz), vmem(2, 2, groups // 4, SUB, nz),
            dma(chunks), dma(chunks), dma(2, chunks, 6), dma(2, chunks, 6), dma(chunks, 6), dma(chunks, 6),
            dma(4, 6), dma(4, 6),
        ],
        compiler_params=pltpu.CompilerParams(collective_id=0, has_side_effects=True, vmem_limit_bytes=48 * 1024 * 1024),
    )(orbitals.reshape(bands, nx * ny, nz), potential.reshape(nx * ny, nz), centre, half_width)
    return out.reshape(bands, nx, ny, nz)


def solution(mesh):
    in_specs = (P(None, "gx", "gy", "gz"), P("gx", "gy", "gz"), P(), P())
    out_specs = P(None, "gx", "gy", "gz")
    return jax.shard_map(local, mesh=mesh, in_specs=in_specs, out_specs=out_specs, check_vma=False)
```

time: 164 us -> 95.9 us (0.58)
  Pallas kernels: 0 us -> 89.3 us
  starting transfers between devices: 65.4 us -> 0 us
  waiting for transfers between devices: 37.5 us -> 0 us
  other arithmetic: 36.1 us -> 0 us
  local copies, waits for them, and re-layouts: 21.5 us -> 4.98 us
    pallas_call x0 -> x1, Pallas kernels: none -> 89.3 us  [local(): pl.pallas_call(functools.partial(kernel, bands, nx, ny, chunks), name='fi...]
    ppermute x42 -> x0, starting transfers between devices: 65.4 us -> none  [the longest x21 47.4 us: extended(): lax.ppermute(leading, axis, [(b, a) for a, b in up])]
    ppermute x42 -> x0, waiting for transfers between devices: 37.5 us -> none  [the longest x21 22.8 us: extended(): lax.ppermute(last, axis, up)]
    div x3 -> x0, other arithmetic: 14.3 us -> none  [the longest x1 14 us: local(): first_order = (first_image - middle * orbitals) / spread]
    sub x2 -> x0, other arithmetic: 12.1 us -> none  [the longest x1 11.8 us: local(): 2.0 * (second_image - middle * first_order) / spread - orbitals]
    slice x21 -> x0, local copies, waits for them, and re-layouts: 5.86 us -> none  [the longest x14 4.68 us: extended(): last = lax.slice_in_dim(array, length - width, length, axis=dim)]
    reduce_sum x4 -> x0, other arithmetic: 5.49 us -> none  [the longest x2 5.15 us: restrict(): field.reshape(shape[0], shape[1] // 2, 2, shape[2] // 2, 2, shape[3] // 2...]
    add x2 -> x0, local copies, waits for them, and re-layouts: 4.49 us -> none  [the longest x1 4.15 us: local(): return second_order + prolong(level_one)]
  transfers between devices with their start and end apart: 42 -> 0, of which waited for: 15 -> 0; matrix products, arithmetic and copies ran while one was open for 5% -> 0% of each run, Pallas kernels for 0% -> 0%
where the time goes in v1:
time: 95.9 us; the launch traced here: 94.3 us
  Pallas kernels  89.3 us (93%)
  local copies, waits for them, and re-layouts  4.98 us (5%)
    pallas_call x1, Pallas kernels, local(): pl.pallas_call(functools.partial(kernel, bands, nx, ny, chunks), name='fi...  89.3 us
    unnamed x9, local copies, waits for them, and re-layouts  4.98 us

profile of v1, /device:TPU:1, one launch (start us, length us, event | category | flops | bytes accessed | tf_op | source)
XLA Modules:
  0.0 94.3 jit_solution(11385561019731138485)
XLA Ops:
  0.0 0.0 copy-start
  0.0 1.6 %copy-done = f32[64,8,8,128]{3,2,1,0:T(8,128)S(1)} copy-done((f32[64,8,8,128]{3,2,1,0:T(8,128)S(1)}, f32[64,8,8,128]{3,2,1,0:T(8,128)}, u32[]{:S(2)}) %copy-start) | copy-done | bytes 2097176
  1.6 0.0 copy-start.1
  1.6 0.8 copy-done.1
  2.4 0.0 copy-start.2
  2.4 0.7 copy-done.2
  3.0 0.0 copy-start.3
  3.0 0.7 copy-done.3
  3.7 89.3 %filter_orbitals.1 = f32[64,64,128]{2,1,0:T(8,128)S(1)} custom-call(f32[64,64,128]{2,1,0:T(8,128)S(1)} %bitcast.4, f32[64,128]{1,0:T(8,128)S(1)} %bitcast.5, f32[64]{0:T(128)S(1)} %copy-done.2, f32[64]{0:T(128)S(1)} %copy-done.3), custom_call_target="tpu_custom_call" | custom-call | tf_op jit(solution)/shard_map/filter_orbitals/pallas_call | solution.py:429
  93.0 1.3 %copy.6 = f32[64,8,8,128]{3,2,1,0:T(8,128)} copy(f32[64,8,8,128]{3,2,1,0:T(8,128)S(1)} %bitcast.3) | data formatting | bytes 4194304
Async XLA Ops:
  0.0 1.6 %copy-start = (f32[64,8,8,128]{3,2,1,0:T(8,128)S(1)}, f32[64,8,8,128]{3,2,1,0:T(8,128)}, u32[]{:S(2)}) copy-start(f32[64,8,8,128]{3,2,1,0:T(8,128)} %param.4) | copy-start | bytes 6291460
  1.6 0.8 copy-start.1
  2.4 0.7 copy-start.2
  3.0 0.7 copy-start.3

commit v2 on v1

v2 whole, which is shorter than its diff:
```python
import functools

import jax
import jax.numpy as jnp
from jax import lax
from jax.experimental import pallas as pl
from jax.experimental.pallas import tpu as pltpu
from jax.sharding import PartitionSpec as P

MESH = pl.DeviceIdType.MESH
shift_mass = 0.05
jacobi_weight = 2.0 / 3.0
SUB, LANES = 8, 128
AXES = ("gx", "gy", "gz")
SIDES = (("gx", 1), ("gx", -1), ("gy", 1), ("gy", -1), ("gz", 1), ("gz", -1))


def lane():
    return lax.broadcasted_iota(jnp.int32, (SUB, LANES), 1)


def sublane():
    return lax.broadcasted_iota(jnp.int32, (SUB, LANES), 0)


def roll(value, shift):
    shift = shift % LANES
    return value if shift == 0 else pltpu.roll(value, shift, 1)


def turn(rows):
    at, rows = sublane(), list(rows)
    for d in (4, 2, 1):
        low = (at & d) == 0
        for i in range(SUB):
            if i & d == 0:
                a, b = rows[i], rows[i + d]
                rows[i] = jnp.where(low, a, pltpu.roll(b, d, 0))
                rows[i + d] = jnp.where(low, pltpu.roll(a, SUB - d, 0), b)
    return rows


def packed(total, value, start, width):
    at = lane()
    moved = roll(value, start + width // 2)
    if total is None:
        return moved
    return jnp.where((at >= start) & (at < start + width), moved, total)


def along_z(value, rims, start, width):
    at, half = lane(), width // 2
    outer = roll(rims, -(start + half))
    left = jnp.where(at < half, outer, roll(value, half))
    right = jnp.where(at >= LANES - half, outer, roll(value, -half))
    return left + right


def met(from_left, from_right, width):
    half = width // 2
    return jnp.where((lane() & half) != 0, roll(from_left, half), roll(from_right, -half))


def pair_sum(value, cell):
    at = lane()
    return value + jnp.where((at & cell) == 0, roll(value, -cell), roll(value, cell))


def kernel(bands, nx, ny, chunks, orb_hbm, pot_hbm, mid_hbm, half_hbm, out_ref,
           stage, pot_ref, mid_ref, half_ref, ZS, TS, A, F, S2, DG, D1, W1, W2, D2, MID, INV, FZS, FZR,
           B1, U1a, U1b, U1c, U2a, U2b, B2, X1S, X1R, Z1S, Z1R, X2S, X2R, Z2S, Z2R,
           in_sem, par_sem, fs, fr, as_, ar, bs, br):
    deep = bands // chunks
    inner = deep // SUB
    groups = bands // SUB
    cx, cy = nx // 2, ny // 2
    ex, ey = nx // 4, ny // 4
    peers = []
    for axis, step in SIDES:
        n = lax.axis_size(axis)
        peers.append({axis: lax.rem(lax.axis_index(axis) + (n + step), n)})

    def load(c):
        part = pl.ds(c * deep, deep)
        return pltpu.make_async_copy(orb_hbm.at[part], stage.at[part], in_sem.at[c])

    params = [pltpu.make_async_copy(a, b, par_sem.at[i])
              for i, (a, b) in enumerate(((pot_hbm, pot_ref), (mid_hbm, mid_ref), (half_hbm, half_ref)))]
    for copy in params:
        copy.start()
    for c in range(chunks):
        load(c).start()
    barrier = pltpu.get_barrier_semaphore()
    for peer in peers:
        pl.semaphore_signal(barrier, inc=1, device_id=peer, device_id_type=MESH)

    def shape(value):
        return jnp.broadcast_to(value, (SUB, LANES))

    for copy in params:
        copy.wait()
    at = sublane()
    for g in range(groups):
        mid = jnp.full((SUB, LANES), mid_ref[g * SUB], jnp.float32)
        half = jnp.full((SUB, LANES), half_ref[g * SUB], jnp.float32)
        for s in range(1, SUB):
            mid = jnp.where(at == s, mid_ref[g * SUB + s], mid)
            half = jnp.where(at == s, half_ref[g * SUB + s], half)
        MID[g] = 6.0 - 2.0 * mid
        INV[g] = 0.5 / half
    ones = {}
    for X in range(cx):
        for Y in range(cy):
            total = None
            for dx in range(2):
                for dy in range(2):
                    k = (2 * X + dx) * ny + 2 * Y + dy
                    row = shape(pot_ref[pl.ds(k, 1), :])
                    DG[k] = 2.0 * row
                    total = row if total is None else total + row
            one = 0.125 * pair_sum(total, 1)
            ones[X, Y] = one
            diagonal = 0.75 + one + shift_mass
            D1[X * cy + Y] = diagonal
            W1[X * cy + Y] = jacobi_weight / diagonal
    for X in range(ex):
        for Y in range(ey):
            total = (ones[2 * X, 2 * Y] + ones[2 * X + 1, 2 * Y]) + (ones[2 * X, 2 * Y + 1] + ones[2 * X + 1, 2 * Y + 1])
            diagonal = 0.1875 + 0.125 * pair_sum(total, 2) + shift_mass
            D2[X * ey + Y] = diagonal
            W2[X * ey + Y] = jacobi_weight / diagonal

    def send(src, dst, s, r, d):
        return pltpu.make_async_remote_copy(
            src_ref=src, dst_ref=dst, send_sem=s, recv_sem=r, device_id=peers[d], device_id_type=MESH)

    def fine(buffer, rnd, c):
        ends = (
            (buffer.at[c, nx, pl.ds(1, ny)], buffer.at[c, 0, pl.ds(1, ny)]),
            (buffer.at[c, 1, pl.ds(1, ny)], buffer.at[c, nx + 1, pl.ds(1, ny)]),
            (buffer.at[c, pl.ds(1, nx), ny], buffer.at[c, pl.ds(1, nx), 0]),
            (buffer.at[c, pl.ds(1, nx), 1], buffer.at[c, pl.ds(1, nx), ny + 1]),
            (FZS.at[rnd, 0, c], FZR.at[rnd, 0, c]),
            (FZS.at[rnd, 1, c], FZR.at[rnd, 1, c]),
        )
        return [send(a, b, fs.at[rnd, c, d], fr.at[rnd, c, d], d) for d, (a, b) in enumerate(ends)]

    def fine_edges(rnd, c, totals):
        odd = (lane() & 1) != 0
        for i in range(inner // 2):
            a, b = totals[2 * i], totals[2 * i + 1]
            FZS[rnd, 0, c, i] = jnp.where(odd, roll(a, 1), b)
            FZS[rnd, 1, c, i] = jnp.where(odd, b, roll(a, -1))

    def fine_rims(rnd, c):
        odd = (lane() & 1) != 0
        rims = []
        for i in range(inner // 2):
            low, high = FZR[rnd, 0, c, i], FZR[rnd, 1, c, i]
            rims.append(jnp.where(odd, low, high))
            rims.append(jnp.where(odd, roll(low, 1), roll(high, -1)))
        return rims

    def start_fine(c):
        load(c).wait()
        totals = [None] * inner
        for j in range(inner):
            for x in range(nx):
                rows = turn([stage[c * deep + j * SUB + i, x * ny:(x + 1) * ny, :] for i in range(SUB)])
                for y in range(ny):
                    A[c, x + 1, y + 1, j * SUB:(j + 1) * SUB, :] = rows[y]
                    totals[j] = packed(totals[j], rows[y], 2 * (x * ny + y), 2)
        fine_edges(0, c, totals)

    def fine_z(buffer, rnd, c):
        rims = fine_rims(rnd, c)
        for j in range(inner):
            band = slice(j * SUB, (j + 1) * SUB)
            for x in range(nx):
                for y in range(ny):
                    k = x * ny + y
                    ZS[k, band, :] = along_z(buffer[c, x + 1, y + 1, band, :], rims[j], 2 * k, 2)

    def apply(buffer, c, x, y, j):
        band = pl.ds(pl.multiple_of(j * SUB, SUB), SUB)
        v = buffer[c, x + 1, y + 1, band, :]
        total = buffer[c, x, y + 1, band, :] + buffer[c, x + 2, y + 1, band, :]
        total = total + buffer[c, x + 1, y, band, :] + buffer[c, x + 1, y + 2, band, :]
        total = total + ZS[x * ny + y, band, :]
        return (DG[x * ny + y] + MID[c * inner + j]) * v - total

    def first_pass(c):
        fine_z(A, 0, c)

        @pl.loop(0, inner)
        def _(j):
            inv = INV[c * inner + j]
            for x in range(nx):
                for y in range(ny):
                    F[c, x + 1, y + 1, pl.ds(pl.multiple_of(j * SUB, SUB), SUB), :] = apply(A, c, x, y, j) * inv

        totals = [None] * inner
        for j in range(inner):
            for x in range(nx):
                for y in range(ny):
                    totals[j] = packed(totals[j], F[c, x + 1, y + 1, j * SUB:(j + 1) * SUB, :], 2 * (x * ny + y), 2)
        fine_edges(1, c, totals)

    def faces(buffer, n, m, tile, count):
        even = (lane() & 1) == 0
        rows = pl.ds(tile, SUB)
        lines = ([(n, y) for y in range(1, m + 1)], [(1, y) for y in range(1, m + 1)],
                 [(x, m) for x in range(1, n + 1)], [(x, 1) for x in range(1, n + 1)])
        return [[jnp.where(even, buffer[l[2 * p][0], l[2 * p][1], rows, :], buffer[l[2 * p + 1][0], l[2 * p + 1][1], rows, :])
                 for p in range(count)] for l in lines]

    def unfaces(buffer, received, rnd, n, m, count, g):
        even = (lane() & 1) == 0
        rows = slice(g * SUB, (g + 1) * SUB)
        lines = ([(0, y) for y in range(1, m + 1)], [(n + 1, y) for y in range(1, m + 1)],
                 [(x, 0) for x in range(1, n + 1)], [(x, m + 1) for x in range(1, n + 1)])
        for d, l in enumerate(lines):
            for p in range(count):
                both = received[rnd, d, p, rows, :]
                buffer[l[2 * p][0], l[2 * p][1], rows, :] = jnp.where(even, both, roll(both, 1))
                buffer[l[2 * p + 1][0], l[2 * p + 1][1], rows, :] = jnp.where(even, roll(both, -1), both)

    def second_pass(c):
        fine_z(F, 1, c)

        @pl.loop(0, inner)
        def _(j):
            band = pl.ds(pl.multiple_of(j * SUB, SUB), SUB)
            scale = 2.0 * INV[c * inner + j]
            for X in range(cx):
                for Y in range(cy):
                    total = None
                    for dx in range(2):
                        for dy in range(2):
                            x, y = 2 * X + dx, 2 * Y + dy
                            value = apply(F, c, x, y, j) * scale - A[c, x + 1, y + 1, band, :]
                            S2[c, x, y, band, :] = value
                            total = value if total is None else total + value
                    TS[X * cy + Y, band, :] = total

        zs = None
        for j in range(inner):
            rows = pl.ds(pl.multiple_of(c * deep + j * SUB, SUB), SUB)
            for X in range(cx):
                for Y in range(cy):
                    source = 0.5 * pair_sum(TS[X * cy + Y, j * SUB:(j + 1) * SUB, :], 1)
                    B1[X * cy + Y, rows, :] = source
                    level = W1[X * cy + Y] * source
                    U1a[X + 1, Y + 1, rows, :] = level
                    zs = packed(zs, level, j * 64 + 4 * (X * cy + Y), 4)
            for d, line in enumerate(faces(U1a, cx, cy, c * deep + j * SUB, cy // 2)):
                for p, value in enumerate(line):
                    X1S[0, d, p, rows, :] = value
        Z1S[0, c] = zs

    def one_chunk(c):
        rows = pl.ds(c * deep, deep)
        copies = [send(X1S.at[0, d, :, rows], X1R.at[0, d, :, rows], as_.at[c, d], ar.at[c, d], d) for d in range(4)]
        return copies + [send(Z1S.at[0, c], Z1R.at[0, d - 4, c], as_.at[c, d], ar.at[c, d], d) for d in (4, 5)]

    def one(rnd):
        k = rnd - 1
        copies = [send(X1S.at[rnd, d], X1R.at[rnd, d], bs.at[k, d], br.at[k, d], d) for d in range(4)]
        return copies + [send(Z1S.at[rnd], Z1R.at[rnd, d - 4], bs.at[k, d], br.at[k, d], d) for d in (4, 5)]

    def two(rnd):
        k = 2 + rnd
        copies = [send(X2S.at[rnd, d], X2R.at[rnd, d], bs.at[k, d], br.at[k, d], d) for d in range(4)]
        return copies + [send(Z2S.at[rnd], Z2R.at[rnd, d - 4], bs.at[k, d], br.at[k, d], d) for d in (4, 5)]

    def tile(g):
        return pl.ds(g * SUB if isinstance(g, int) else pl.multiple_of(g * SUB, SUB), SUB)

    def coarse_z(buffer, received, rnd, n, m, width):
        per = LANES // (n * m * width)
        for g in range(groups):
            rims = met(received[rnd, 0, g // per], received[rnd, 1, g // per], width)
            for X in range(n):
                for Y in range(m):
                    start = (g % per) * n * m * width + width * (X * m + Y)
                    ZS[X * m + Y, tile(g), :] = along_z(buffer[X + 1, Y + 1, tile(g), :], rims, start, width)

    def coarse_edges(buffer, out, rnd, n, m, width):
        per = LANES // (n * m * width)
        for g in range(groups):
            zs = None if g % per == 0 else zs
            for X in range(n):
                for Y in range(m):
                    start = (g % per) * n * m * width + width * (X * m + Y)
                    zs = packed(zs, buffer[X + 1, Y + 1, tile(g), :], start, width)
            if g % per == per - 1:
                out[rnd, g // per] = zs

    def around(buffer, X, Y, m, g):
        rows = tile(g)
        u = buffer[X + 1, Y + 1, rows, :]
        total = buffer[X, Y + 1, rows, :] + buffer[X + 2, Y + 1, rows, :]
        total = total + buffer[X + 1, Y, rows, :] + buffer[X + 1, Y + 2, rows, :]
        return u, total + ZS[X * m + Y, rows, :]

    def send_faces(buffer, out, rnd, n, m, g):
        rows = tile(g)
        for d, line in enumerate(faces(buffer, n, m, rows.start, m // 2)):
            for p, value in enumerate(line):
                out[rnd, d, p, rows, :] = value

    def sweep_one(buffer, g, X, Y):
        u, total = around(buffer, X, Y, cy, g)
        return u * (1.0 - jacobi_weight) + W1[X * cy + Y] * (B1[X * cy + Y, tile(g), :] + 0.125 * total)

    def sweep_two(buffer, g, X, Y):
        u, total = around(buffer, X, Y, ey, g)
        return u * (1.0 - jacobi_weight) + W2[X * ey + Y] * (B2[X * ey + Y, tile(g), :] + 0.03125 * total)

    with jax.named_scope('barrier'):
        pl.semaphore_wait(barrier, 6)

    @pl.loop(0, chunks)
    def _(c):
        with jax.named_scope('load'):
            start_fine(c)
        for copy in fine(A, 0, c):
            copy.start()

    @pl.loop(0, chunks)
    def _(c):
        with jax.named_scope('w0'):
            for copy in fine(A, 0, c):
                copy.wait_recv()
        with jax.named_scope('first'):
            first_pass(c)
        for copy in fine(F, 1, c):
            copy.start()

    @pl.loop(0, chunks)
    def _(c):
        with jax.named_scope('w1'):
            for copy in fine(F, 1, c):
                copy.wait_recv()
        with jax.named_scope('second'):
            second_pass(c)
        for copy in one_chunk(c):
            copy.start()

    with jax.named_scope('w2'):
        for c in range(chunks):
            for copy in one_chunk(c):
                copy.wait_recv()
    for g in range(groups):
        unfaces(U1a, X1R, 0, cx, cy, cy // 2, g)
    coarse_z(U1a, Z1R, 0, cx, cy, 4)

    @pl.loop(0, groups)
    def _(g):
        for X in range(cx):
            for Y in range(cy):
                U1b[X + 1, Y + 1, tile(g), :] = sweep_one(U1a, g, X, Y)
        send_faces(U1b, X1S, 1, cx, cy, g)

    coarse_edges(U1b, Z1S, 1, cx, cy, 4)
    for copy in one(1):
        copy.start()
    with jax.named_scope('w3'):
        for copy in one(1):
            copy.wait_recv()
    for g in range(groups):
        unfaces(U1b, X1R, 1, cx, cy, cy // 2, g)
    coarse_z(U1b, Z1R, 1, cx, cy, 4)

    @pl.loop(0, groups)
    def _(g):
        for X in range(ex):
            for Y in range(ey):
                sums = None
                for dx in range(2):
                    for dy in range(2):
                        x, y = 2 * X + dx, 2 * Y + dy
                        u, total = around(U1b, x, y, cy, g)
                        residue = B1[x * cy + y, tile(g), :] - D1[x * cy + y] * u + 0.125 * total
                        sums = residue if sums is None else sums + residue
                B2[X * ey + Y, tile(g), :] = sums

    for g in range(groups):
        for X in range(ex):
            for Y in range(ey):
                source = 0.5 * pair_sum(B2[X * ey + Y, tile(g), :], 2)
                B2[X * ey + Y, tile(g), :] = source
                U2a[X + 1, Y + 1, tile(g), :] = W2[X * ey + Y] * source
        send_faces(U2a, X2S, 0, ex, ey, g)
    coarse_edges(U2a, Z2S, 0, ex, ey, 8)
    for copy in two(0):
        copy.start()
    with jax.named_scope('w4'):
        for copy in two(0):
            copy.wait_recv()
    for g in range(groups):
        unfaces(U2a, X2R, 0, ex, ey, ey // 2, g)
    coarse_z(U2a, Z2R, 0, ex, ey, 8)

    @pl.loop(0, groups)
    def _(g):
        for X in range(ex):
            for Y in range(ey):
                U2b[X + 1, Y + 1, tile(g), :] = sweep_two(U2a, g, X, Y)
        send_faces(U2b, X2S, 1, ex, ey, g)

    coarse_edges(U2b, Z2S, 1, ex, ey, 8)
    for copy in two(1):
        copy.start()
    with jax.named_scope('w5'):
        for copy in two(1):
            copy.wait_recv()
    for g in range(groups):
        unfaces(U2b, X2R, 1, ex, ey, ey // 2, g)
    coarse_z(U2b, Z2R, 1, ex, ey, 8)

    @pl.loop(0, groups)
    def _(g):
        for X in range(ex):
            for Y in range(ey):
                value = sweep_two(U2b, g, X, Y)
                for dx in range(2):
                    for dy in range(2):
                        x, y = 2 * X + dx, 2 * Y + dy
                        U1c[x + 1, y + 1, tile(g), :] = U1b[x + 1, y + 1, tile(g), :] + value
        send_faces(U1c, X1S, 2, cx, cy, g)

    coarse_edges(U1c, Z1S, 2, cx, cy, 4)
    for copy in one(2):
        copy.start()
    with jax.named_scope('w6'):
        for copy in one(2):
            copy.wait_recv()
    for g in range(groups):
        unfaces(U1c, X1R, 2, cx, cy, cy // 2, g)
    coarse_z(U1c, Z1R, 2, cx, cy, 4)

    @pl.loop(0, groups)
    def _(g):
        c, j = g // inner, g % inner
        band = pl.ds(pl.multiple_of(j * SUB, SUB), SUB)
        for X in range(cx):
            levels = [sweep_one(U1c, g, X, Y) for Y in range(cy)]
            for x in (2 * X, 2 * X + 1):
                values = turn([S2[c, x, y, band, :] + levels[y // 2] for y in range(ny)])
                for i in range(SUB):
                    out_ref[g * SUB + i, x * ny:(x + 1) * ny, :] = values[i]

    with jax.named_scope('sent'):
        for c in range(chunks):
            for copy in fine(A, 0, c) + fine(F, 1, c) + one_chunk(c):
                copy.wait_send()
        for copy in one(1) + one(2) + two(0) + two(1):
            copy.wait_send()


def local(orbitals, potential, centre, half_width):
    bands, nx, ny, nz = orbitals.shape
    chunks = 4
    deep = bands // chunks
    cx, cy, ex, ey = nx // 2, ny // 2, nx // 4, ny // 4
    groups = bands // SUB
    vmem = lambda *s: pltpu.VMEM(s, jnp.float32)
    dma = lambda *s: pltpu.SemaphoreType.DMA(s)
    out = pl.pallas_call(
        functools.partial(kernel, bands, nx, ny, chunks),
        name="filter_orbitals",
        out_shape=jax.ShapeDtypeStruct((bands, nx * ny, nz), jnp.float32),
        in_specs=[pl.BlockSpec(memory_space=pltpu.HBM)] * 4,
        out_specs=pl.BlockSpec(memory_space=pltpu.VMEM),
        scratch_shapes=[
            vmem(bands, nx * ny, nz), vmem(nx * ny, nz), pltpu.SMEM((bands,), jnp.float32), pltpu.SMEM((bands,), jnp.float32),
            vmem(nx * ny, bands, nz), vmem(cx * cy, deep, nz),
            vmem(chunks, nx + 2, ny + 2, deep, nz), vmem(chunks, nx + 2, ny + 2, deep, nz), vmem(chunks, nx, ny, deep, nz),
            vmem(nx * ny, SUB, nz), vmem(cx * cy, SUB, nz), vmem(cx * cy, SUB, nz), vmem(ex * ey, SUB, nz), vmem(ex * ey, SUB, nz),
            vmem(groups, SUB, nz), vmem(groups, SUB, nz),
            vmem(2, 2, chunks, deep // 16, SUB, nz), vmem(2, 2, chunks, deep // 16, SUB, nz),
            vmem(cx * cy, bands, nz),
            vmem(cx + 2, cy + 2, bands, nz), vmem(cx + 2, cy + 2, bands, nz), vmem(cx + 2, cy + 2, bands, nz),
            vmem(ex + 2, ey + 2, bands, nz), vmem(ex + 2, ey + 2, bands, nz), vmem(ex * ey, bands, nz),
            vmem(3, 4, cy // 2, bands, nz), vmem(3, 4, cy // 2, bands, nz),
            vmem(3, groups // 2, SUB, nz), vmem(3, 2, groups // 2, SUB, nz),
            vmem(2, 4, ey // 2, bands, nz), vmem(2, 4, ey // 2, bands, nz),
            vmem(2, groups // 4, SUB, nz), vmem(2, 2, groups // 4, SUB, nz),
            dma(chunks), dma(3), dma(2, chunks, 6), dma(2, chunks, 6), dma(chunks, 6), dma(chunks, 6),
            dma(4, 6), dma(4, 6),
        ],
        compiler_params=pltpu.CompilerParams(collective_id=0, has_side_effects=True, vmem_limit_bytes=48 * 1024 * 1024),
    )(*(pltpu.with_memory_space_constraint(a, pltpu.HBM) for a in (orbitals.reshape(bands, nx * ny, nz), potential.reshape(nx * ny, nz), centre, half_width)))
    return out.reshape(bands, nx, ny, nz)


def solution(mesh):
    in_specs = (P(None, "gx", "gy", "gz"), P("gx", "gy", "gz"), P(), P())
    out_specs = P(None, "gx", "gy", "gz")
    return jax.shard_map(local, mesh=mesh, in_specs=in_specs, out_specs=out_specs, check_vma=False)
```

time: 95.9 us -> 59.9 us (0.62)
  the two profiles are of different devices: /device:TPU:1 before, /device:TPU:0 now
where the time goes in v2:
time: 59.9 us; the launch traced here: 59.7 us
  Pallas kernels  58.4 us (97%)
  local copies, waits for them, and re-layouts  1.32 us (2%)
    pallas_call x1, Pallas kernels, local(): pl.pallas_call(functools.partial(kernel, bands, nx, ny, chunks), name='fi...  58.4 us
    unnamed x1, local copies, waits for them, and re-layouts  1.32 us

profile of v2, /device:TPU:0, one launch (start us, length us, event | category | flops | bytes accessed | tf_op | source)
XLA Modules:
  0.0 59.7 jit_solution(7151074936511476073)
XLA Ops:
  0.0 58.4 %filter_orbitals.1 = f32[64,64,128]{2,1,0:T(8,128)S(1)} custom-call(f32[64,64,128]{2,1,0:T(8,128)} %bitcast.4, f32[64,128]{1,0:T(8,128)} %bitcast.5, f32[64]{0:T(128)} %mid_hbm.1, f32[64]{0:T(128)} %half_hbm.1), custom_call_target="tpu_custom_call" | custom-call | tf_op jit(solution)/shard_map/filter_orbitals/pallas_call | solution.py:470
  58.4 1.3 %copy.6 = f32[64,8,8,128]{3,2,1,0:T(8,128)} copy(f32[64,8,8,128]{3,2,1,0:T(8,128)S(1)} %bitcast.3) | data formatting | bytes 4194304

commit v3 on v2

v3 whole, which is shorter than its diff:
```python
import functools

import jax
import jax.numpy as jnp
from jax import lax
from jax.experimental import pallas as pl
from jax.experimental.pallas import tpu as pltpu
from jax.sharding import PartitionSpec as P

MESH = pl.DeviceIdType.MESH
shift_mass = 0.05
jacobi_weight = 2.0 / 3.0
SUB, LANES = 8, 128
AXES = ("gx", "gy", "gz")
SIDES = (("gx", 1), ("gx", -1), ("gy", 1), ("gy", -1), ("gz", 1), ("gz", -1))
RING = ((1, 0), (-1, 0), (0, 1), (0, -1), (1, 1), (1, -1), (-1, 1), (-1, -1), (2, 0), (0, 2))
NEAR = RING[:8]
CROSS = RING[:4]
EDGE = 16


def lane():
    return lax.broadcasted_iota(jnp.int32, (SUB, LANES), 1)


def sublane():
    return lax.broadcasted_iota(jnp.int32, (SUB, LANES), 0)


def roll(value, shift):
    shift = shift % LANES
    return value if shift == 0 else pltpu.roll(value, shift, 1)


def turn(rows):
    at, rows = sublane(), list(rows)
    for d in (4, 2, 1):
        low = (at & d) == 0
        for i in range(SUB):
            if i & d == 0:
                a, b = rows[i], rows[i + d]
                rows[i] = jnp.where(low, a, pltpu.roll(b, d, 0))
                rows[i + d] = jnp.where(low, pltpu.roll(a, SUB - d, 0), b)
    return rows


def woven(columns):
    at = lane() & 3
    total = columns[3]
    for q in range(3):
        total = jnp.where(at == q, columns[q], total)
    return total


def spread(low, high, q):
    at = lane() & 3
    total = roll(high, 3 - q)
    for i, value in ((0, low), (1, low), (2, high)):
        total = jnp.where(at == i, roll(value, i - q), total)
    return total


def beside(own, low, high, bit):
    return jnp.where((lane() & bit) == 0, roll(own + low, -bit), roll(own + high, bit))


def below(main, other):
    return jnp.where(lane() < 4, roll(other, 4), roll(main, 4))


def above(main, other):
    return jnp.where(lane() >= LANES - 4, roll(other, -4), roll(main, -4))


def packed(total, value, start, width):
    at = lane()
    moved = roll(value, start + width // 2)
    if total is None:
        return moved
    return jnp.where((at >= start) & (at < start + width), moved, total)


def along_z(value, rims, start, width):
    at, half = lane(), width // 2
    outer = roll(rims, -(start + half))
    left = jnp.where(at < half, outer, roll(value, half))
    right = jnp.where(at >= LANES - half, outer, roll(value, -half))
    return left + right


def met(from_left, from_right, width):
    half = width // 2
    return jnp.where((lane() & half) != 0, roll(from_left, half), roll(from_right, -half))


def pair_sum(value, cell):
    at = lane()
    return value + jnp.where((at & cell) == 0, roll(value, -cell), roll(value, cell))


def kernel(bands, nx, ny, chunks, orb_hbm, pot_hbm, mid_hbm, half_hbm, out_ref,
           stage, pot_ref, mid_ref, half_ref, ZS, TS, A, F, S2, DG, D1, W1, MID, INV, FZS, FZR,
           B1, U1a, U1b, B2, X1S, X1R, Z1S, Z1R, MPS, MPR, WPS, WPR, EPS, EPR, XPR, XE, PA, PB, TT, TZ,
           in_sem, par_sem, sent, fine_got, one_got, got, got_w):
    deep = bands // chunks
    inner = deep // SUB
    groups = bands // SUB
    halves = 2
    share = groups // halves
    cx, cy = nx // 2, ny // 2
    ex, ey = nx // 4, ny // 4
    peers = []
    for axis, step in SIDES:
        n = lax.axis_size(axis)
        peers.append({axis: lax.rem(lax.axis_index(axis) + (n + step), n)})
    around_xy = []
    for step in RING:
        place = {}
        for axis, k in zip(AXES, step):
            n = lax.axis_size(axis)
            place[axis] = lax.rem(lax.axis_index(axis) + (n + k), n)
        around_xy.append(place)

    def load(c):
        part = pl.ds(c * deep, deep)
        return pltpu.make_async_copy(orb_hbm.at[part], stage.at[part], in_sem.at[c])

    params = [pltpu.make_async_copy(a, b, par_sem.at[i])
              for i, (a, b) in enumerate(((pot_hbm, pot_ref), (mid_hbm, mid_ref), (half_hbm, half_ref)))]
    for copy in params:
        copy.start()
    for c in range(chunks):
        load(c).start()
    barrier = pltpu.get_barrier_semaphore()
    for peer in peers + around_xy[4:]:
        pl.semaphore_signal(barrier, inc=1, device_id=peer, device_id_type=MESH)

    def shape(value):
        return jnp.broadcast_to(value, (SUB, LANES))

    def prologue():
        for copy in params:
            copy.wait()
        at = sublane()
        for g in range(groups):
            mid = jnp.full((SUB, LANES), mid_ref[g * SUB], jnp.float32)
            half = jnp.full((SUB, LANES), half_ref[g * SUB], jnp.float32)
            for s in range(1, SUB):
                mid = jnp.where(at == s, mid_ref[g * SUB + s], mid)
                half = jnp.where(at == s, half_ref[g * SUB + s], half)
            MID[g] = 6.0 - 2.0 * mid
            INV[g] = 0.5 / half
        ones = {}
        for X in range(cx):
            for Y in range(cy):
                total = None
                for dx in range(2):
                    for dy in range(2):
                        k = (2 * X + dx) * ny + 2 * Y + dy
                        row = shape(pot_ref[pl.ds(k, 1), :])
                        DG[k] = 2.0 * row
                        total = row if total is None else total + row
                one = 0.125 * pair_sum(total, 1)
                ones[X, Y] = one
                diagonal = 0.75 + one + shift_mass
                D1[X * cy + Y] = diagonal
                W1[X * cy + Y] = jacobi_weight / diagonal
        two_diagonals = []
        for X in range(ex):
            for Y in range(ey):
                total = (ones[2 * X, 2 * Y] + ones[2 * X + 1, 2 * Y]) + (ones[2 * X, 2 * Y + 1] + ones[2 * X + 1, 2 * Y + 1])
                diagonal = 0.1875 + 0.125 * pair_sum(total, 2) + shift_mass
                two_diagonals.append(jacobi_weight / diagonal)
        WPS[...] = woven(two_diagonals)

    def send(src, dst, s, r, d):
        return pltpu.make_async_remote_copy(
            src_ref=src, dst_ref=dst, send_sem=s, recv_sem=r, device_id=peers[d], device_id_type=MESH)

    def fine(buffer, rnd, c):
        ends = (
            (buffer.at[c, nx, pl.ds(1, ny)], buffer.at[c, 0, pl.ds(1, ny)]),
            (buffer.at[c, 1, pl.ds(1, ny)], buffer.at[c, nx + 1, pl.ds(1, ny)]),
            (buffer.at[c, pl.ds(1, nx), ny], buffer.at[c, pl.ds(1, nx), 0]),
            (buffer.at[c, pl.ds(1, nx), 1], buffer.at[c, pl.ds(1, nx), ny + 1]),
            (FZS.at[rnd, 0, c], FZR.at[rnd, 0, c]),
            (FZS.at[rnd, 1, c], FZR.at[rnd, 1, c]),
        )
        return [send(a, b, sent.at[d // 4], fine_got.at[rnd, c, d // 4], d) for d, (a, b) in enumerate(ends)]

    def whole(ref, sem):
        pltpu.make_async_copy(ref, ref, sem).wait()

    def fine_wait(rnd, c):
        whole(stage.at[pl.ds(0, 2 * deep * (nx + ny) // (nx * ny))], fine_got.at[rnd, c, 0])
        whole(FZR.at[rnd, :, c], fine_got.at[rnd, c, 1])

    def fine_edges(rnd, c, totals):
        odd = (lane() & 1) != 0
        for i in range(inner // 2):
            a, b = totals[2 * i], totals[2 * i + 1]
            FZS[rnd, 0, c, i] = jnp.where(odd, roll(a, 1), b)
            FZS[rnd, 1, c, i] = jnp.where(odd, b, roll(a, -1))

    def fine_rims(rnd, c):
        odd = (lane() & 1) != 0
        rims = []
        for i in range(inner // 2):
            low, high = FZR[rnd, 0, c, i], FZR[rnd, 1, c, i]
            rims.append(jnp.where(odd, low, high))
            rims.append(jnp.where(odd, roll(low, 1), roll(high, -1)))
        return rims

    def start_fine(c):
        load(c).wait()
        totals = [None] * inner
        for j in range(inner):
            for x in range(nx):
                rows = turn([stage[c * deep + j * SUB + i, x * ny:(x + 1) * ny, :] for i in range(SUB)])
                for y in range(ny):
                    A[c, x + 1, y + 1, j * SUB:(j + 1) * SUB, :] = rows[y]
                    totals[j] = packed(totals[j], rows[y], 2 * (x * ny + y), 2)
        fine_edges(0, c, totals)

    def fine_z(buffer, rnd, c):
        rims = fine_rims(rnd, c)
        for j in range(inner):
            band = slice(j * SUB, (j + 1) * SUB)
            for x in range(nx):
                for y in range(ny):
                    k = x * ny + y
                    ZS[k, band, :] = along_z(buffer[c, x + 1, y + 1, band, :], rims[j], 2 * k, 2)

    def apply(buffer, c, x, y, j):
        band = pl.ds(pl.multiple_of(j * SUB, SUB), SUB)
        v = buffer[c, x + 1, y + 1, band, :]
        total = buffer[c, x, y + 1, band, :] + buffer[c, x + 2, y + 1, band, :]
        total = total + buffer[c, x + 1, y, band, :] + buffer[c, x + 1, y + 2, band, :]
        total = total + ZS[x * ny + y, band, :]
        return (DG[x * ny + y] + MID[c * inner + j]) * v - total

    def first_pass(c):
        fine_z(A, 0, c)

        @pl.loop(0, inner)
        def _(j):
            inv = INV[c * inner + j]
            for x in range(nx):
                for y in range(ny):
                    F[c, x + 1, y + 1, pl.ds(pl.multiple_of(j * SUB, SUB), SUB), :] = apply(A, c, x, y, j) * inv

        totals = [None] * inner
        for j in range(inner):
            for x in range(nx):
                for y in range(ny):
                    totals[j] = packed(totals[j], F[c, x + 1, y + 1, j * SUB:(j + 1) * SUB, :], 2 * (x * ny + y), 2)
        fine_edges(1, c, totals)

    def faces(buffer, n, m, tile, count):
        even = (lane() & 1) == 0
        rows = pl.ds(tile, SUB)
        lines = ([(n, y) for y in range(1, m + 1)], [(1, y) for y in range(1, m + 1)],
                 [(x, m) for x in range(1, n + 1)], [(x, 1) for x in range(1, n + 1)])
        return [[jnp.where(even, buffer[l[2 * p][0], l[2 * p][1], rows, :], buffer[l[2 * p + 1][0], l[2 * p + 1][1], rows, :])
                 for p in range(count)] for l in lines]

    def unfaces(buffer, received, rnd, n, m, count, g):
        even = (lane() & 1) == 0
        rows = tile(g)
        lines = ([(0, y) for y in range(1, m + 1)], [(n + 1, y) for y in range(1, m + 1)],
                 [(x, 0) for x in range(1, n + 1)], [(x, m + 1) for x in range(1, n + 1)])
        for d, l in enumerate(lines):
            for p in range(count):
                both = received[rnd, d, p, rows, :]
                buffer[l[2 * p][0], l[2 * p][1], rows, :] = jnp.where(even, both, roll(both, 1))
                buffer[l[2 * p + 1][0], l[2 * p + 1][1], rows, :] = jnp.where(even, roll(both, -1), both)

    def second_pass(c):
        fine_z(F, 1, c)

        @pl.loop(0, inner)
        def _(j):
            band = pl.ds(pl.multiple_of(j * SUB, SUB), SUB)
            scale = 2.0 * INV[c * inner + j]
            for X in range(cx):
                for Y in range(cy):
                    total = None
                    for dx in range(2):
                        for dy in range(2):
                            x, y = 2 * X + dx, 2 * Y + dy
                            value = apply(F, c, x, y, j) * scale - A[c, x + 1, y + 1, band, :]
                            S2[c, x, y, band, :] = value
                            total = value if total is None else total + value
                    TS[X * cy + Y, band, :] = total

        zs = None
        for j in range(inner):
            rows = pl.ds(pl.multiple_of(c * deep + j * SUB, SUB), SUB)
            for X in range(cx):
                for Y in range(cy):
                    source = 0.5 * pair_sum(TS[X * cy + Y, j * SUB:(j + 1) * SUB, :], 1)
                    B1[X * cy + Y, rows, :] = source
                    level = W1[X * cy + Y] * source
                    U1a[X + 1, Y + 1, rows, :] = level
                    zs = packed(zs, level, j * 64 + 4 * (X * cy + Y), 4)
            for d, line in enumerate(faces(U1a, cx, cy, c * deep + j * SUB, cy // 2)):
                for p, value in enumerate(line):
                    X1S[0, d, p, rows, :] = value
        Z1S[0, c] = zs

    def one(rnd, c):
        rows = pl.ds(pl.multiple_of(c * deep, deep), deep)
        copies = [send(X1S.at[rnd, d, :, rows], X1R.at[rnd, d, :, rows], sent.at[2], one_got.at[rnd, c, 0], d)
                  for d in range(4)]
        return copies + [send(Z1S.at[rnd, c], Z1R.at[rnd, d - 4, c], sent.at[3], one_got.at[rnd, c, 1], d) for d in (4, 5)]

    def one_wait(rnd, c):
        rows = pl.ds(pl.multiple_of(c * deep, deep), deep)
        whole(X1R.at[rnd, :, :, rows], one_got.at[rnd, c, 0])
        whole(Z1R.at[rnd, :, c], one_got.at[rnd, c, 1])

    def slot(step):
        return RING.index(step) if step in RING else RING.index((abs(step[0]), abs(step[1])))

    def remote(src, dst, s, r, place):
        return pltpu.make_async_remote_copy(
            src_ref=src, dst_ref=dst, send_sem=s, recv_sem=r, device_id=place, device_id_type=MESH)

    def gather(h):
        copies = []
        for i, (a, b) in enumerate(RING):
            copies.append(remote(MPS.at[h], MPR.at[h, slot((-a, -b))], sent.at[4], got.at[h, 0], around_xy[i]))
        return copies

    def gather_diagonal():
        copies = []
        for i, (a, b) in enumerate(RING):
            copies.append(remote(WPS, WPR.at[slot((-a, -b))], sent.at[5], got_w, around_xy[i]))
        return copies

    def ends(h):
        return [send(EPS.at[h, d], EPR.at[h, d], sent.at[6], got.at[h, 1], 4 + d) for d in range(2)]

    def forward(h):
        copies = []
        for i, (a, b) in enumerate(NEAR):
            copies.append(remote(EPR.at[h], XPR.at[h, slot((-a, -b))], sent.at[7], got.at[h, 2], around_xy[i]))
        return copies

    def tile(g):
        return pl.ds(g * SUB if isinstance(g, int) else pl.multiple_of(g * SUB, SUB), SUB)

    def coarse_z(buffer, rnd, c):
        rims = met(Z1R[rnd, 0, c], Z1R[rnd, 1, c], 4)
        for j in range(inner):
            for X in range(cx):
                for Y in range(cy):
                    k = X * cy + Y
                    value = buffer[X + 1, Y + 1, tile(c * inner + j), :]
                    ZS[k, tile(c * inner + j), :] = along_z(value, rims, 4 * (j * cx * cy + k), 4)

    def coarse_edges(buffer, rnd, c):
        zs = None
        for j in range(inner):
            for X in range(cx):
                for Y in range(cy):
                    zs = packed(zs, buffer[X + 1, Y + 1, tile(c * inner + j), :], 4 * (j * cx * cy + X * cy + Y), 4)
        Z1S[rnd, c] = zs

    def around(buffer, X, Y, m, g):
        rows = tile(g)
        u = buffer[X + 1, Y + 1, rows, :]
        total = buffer[X, Y + 1, rows, :] + buffer[X + 2, Y + 1, rows, :]
        total = total + buffer[X + 1, Y, rows, :] + buffer[X + 1, Y + 2, rows, :]
        return u, total + ZS[X * m + Y, rows, :]

    def send_faces(buffer, out, rnd, n, m, g):
        rows = tile(g)
        for d, line in enumerate(faces(buffer, n, m, rows.start, m // 2)):
            for p, value in enumerate(line):
                out[rnd, d, p, rows, :] = value

    def sweep_one(buffer, g, X, Y):
        u, total = around(buffer, X, Y, cy, g)
        return u * (1.0 - jacobi_weight) + W1[X * cy + Y] * (B1[X * cy + Y, tile(g), :] + 0.125 * total)

    def level_two(h):
        at = lane()
        for b in range(9):
            low, high = (EPR[h, 0], EPR[h, 1]) if b == 8 else (XPR[h, b, 0], XPR[h, b, 1])
            for g in range(share + 1):
                XE[b, g] = jnp.where(at < EDGE, roll(high, -EDGE * g), roll(low, LANES - EDGE - EDGE * g))

        def main(step, g):
            if isinstance(g, int) and g == share:
                return WPS[...] if step == (0, 0) else WPR[slot(step)]
            return MPS[h, g] if step == (0, 0) else MPR[h, slot(step), g]

        def edge(step, g):
            return XE[8 if step == (0, 0) else slot(step), g]

        def know(step):
            return step == (0, 0) or step in RING or (abs(step[0]), abs(step[1])) in RING

        def total(value, other, near):
            x = beside(value, near(-1, 0), near(1, 0), 2)
            y = beside(value, near(0, -1), near(0, 1), 1)
            return x + y + (below(value, other) + above(value, other))

        own = (0, 0)
        first_main = (own,) + NEAR
        first_edge = (own,) + CROSS
        for g in range(share):
            start = {}
            for step in first_main + RING[8:]:
                start[step, 0] = main(step, share) * main(step, g)
            for step in first_main:
                start[step, 1] = edge(step, share) * edge(step, g)

            def near_of(step, part, value):
                def near(a, b):
                    there = (step[0] + a, step[1] + b)
                    there = there if know(there) else step
                    there = there if there == own or there in RING else (abs(there[0]), abs(there[1]))
                    return start.get((there, part), value)
                return near

            for n, step in enumerate(first_main):
                value, other = start[step, 0], start[step, 1]
                PA[g, n] = total(value, other, near_of(step, 0, value))
            for n, step in enumerate(first_edge):
                value, other = start[step, 1], start[step, 0]
                PA[g, 9 + n] = total(value, other, near_of(step, 1, value))

        @pl.loop(0, share)
        def _(g):
            for n, step in enumerate(first_main):
                w, b = main(step, share), main(step, g)
                PB[g, n] = (w * b) * (1.0 - jacobi_weight) + w * (b + 0.03125 * PA[g, n])
            for n, step in enumerate(first_edge):
                w, b = edge(step, share), edge(step, g)
                PB[g, 9 + n] = (w * b) * (1.0 - jacobi_weight) + w * (b + 0.03125 * PA[g, 9 + n])

        for g in range(share):
            def near_of(step, part, value):
                def near(a, b):
                    there = (step[0] + a, step[1] + b)
                    known = first_main if part == 0 else first_edge
                    return PB[g, 9 * part + known.index(there)] if there in known else value
                return near

            for n, step in enumerate(first_edge):
                value, other = PB[g, n], PB[g, 9 + n]
                PA[g, n] = total(value, other, near_of(step, 0, value))
            value, other = PB[g, 9], PB[g, 0]
            PA[g, 9] = total(value, other, near_of(own, 1, value))

        @pl.loop(0, share)
        def _(g):
            for n, step in enumerate(first_edge):
                w, b = main(step, share), main(step, g)
                PB[g, n] = PB[g, n] * (1.0 - jacobi_weight) + w * (b + 0.03125 * PA[g, n])
            w, b = edge(own, share), edge(own, g)
            PB[g, 9] = PB[g, 9] * (1.0 - jacobi_weight) + w * (b + 0.03125 * PA[g, 9])

        for g in range(share):
            value, other = PB[g, 0], PB[g, 9]
            PA[g, 0] = below(value, other)
            PA[g, 1] = above(value, other)
            for X in range(ex):
                for Y in range(ey):
                    TT[X + 1, Y + 1, tile(h * share + g), :] = spread(value, value, 2 * X + Y)
            for n, (a, b) in enumerate(CROSS):
                value = PB[g, 1 + n]
                for k in range(2):
                    X, Y = (k, 0) if a == 0 else (0, k)
                    X, Y = (1 if a < 0 else X), (1 if b < 0 else Y)
                    TT[2 * a + X + 1, 2 * b + Y + 1, tile(h * share + g), :] = spread(value, value, 2 * X + Y)
        for g in range(share):
            for q in range(ex * ey):
                TZ[q, tile(h * share + g), :] = spread(PA[g, 0], PA[g, 1], q)

    with jax.named_scope('barrier'):
        pl.semaphore_wait(barrier, 12)

    @pl.loop(0, chunks)
    def _(c):
        with jax.named_scope('load'):
            start_fine(c)
        for copy in fine(A, 0, c):
            copy.start()

    with jax.named_scope('prologue'):
        prologue()
    for copy in gather_diagonal():
        copy.start()

    @pl.loop(0, chunks)
    def _(c):
        with jax.named_scope('w0'):
            fine_wait(0, c)
        with jax.named_scope('first'):
            first_pass(c)
        for copy in fine(F, 1, c):
            copy.start()

    @pl.loop(0, chunks)
    def _(c):
        with jax.named_scope('w1'):
            fine_wait(1, c)
        with jax.named_scope('second'):
            second_pass(c)
        for copy in one(0, c):
            copy.start()

    @pl.loop(0, chunks)
    def _(c):
        with jax.named_scope('w2'):
            one_wait(0, c)
        with jax.named_scope('sweep'):
            for j in range(inner):
                unfaces(U1a, X1R, 0, cx, cy, cy // 2, c * inner + j)
            coarse_z(U1a, 0, c)

            @pl.loop(0, inner)
            def _(j):
                g = c * inner + j
                for X in range(cx):
                    for Y in range(cy):
                        U1b[X + 1, Y + 1, tile(g), :] = sweep_one(U1a, g, X, Y)
                send_faces(U1b, X1S, 1, cx, cy, g)

            coarse_edges(U1b, 1, c)
        for copy in one(1, c):
            copy.start()

    @pl.loop(0, halves)
    def _(h):
        @pl.loop(0, chunks // halves)
        def _(i):
            c = h * (chunks // halves) + i
            with jax.named_scope('w3'):
                one_wait(1, c)
            with jax.named_scope('residue'):
                for j in range(inner):
                    unfaces(U1b, X1R, 1, cx, cy, cy // 2, c * inner + j)
                coarse_z(U1b, 1, c)

                @pl.loop(0, inner)
                def _(j):
                    g = c * inner + j
                    for X in range(ex):
                        for Y in range(ey):
                            sums = None
                            for dx in range(2):
                                for dy in range(2):
                                    x, y = 2 * X + dx, 2 * Y + dy
                                    u, total = around(U1b, x, y, cy, g)
                                    residue = B1[x * cy + y, tile(g), :] - D1[x * cy + y] * u + 0.125 * total
                                    B1[x * cy + y, tile(g), :] = residue
                                    sums = residue if sums is None else sums + residue
                            B2[X * ey + Y, tile(g), :] = sums

        with jax.named_scope('weave'):
            parts = []
            for g in range(share):
                part = woven([0.5 * pair_sum(B2[q, tile(h * share + g), :], 2) for q in range(ex * ey)])
                MPS[h, g] = part
                parts.append(part)
            parts.append(WPS[...])
            low = high = None
            for g, part in enumerate(parts):
                here = (lane() >= EDGE * g) & (lane() < EDGE * (g + 1))
                up, down = roll(part, EDGE * g + EDGE), roll(part, EDGE * g)
                high = up if high is None else jnp.where(here, up, high)
                low = down if low is None else jnp.where(here, down, low)
            EPS[h, 0], EPS[h, 1] = high, low
        for copy in ends(h) + gather(h):
            copy.start()

    @pl.loop(0, halves)
    def _(h):
        with jax.named_scope('w4'):
            whole(EPR.at[h], got.at[h, 1])
        for copy in forward(h):
            copy.start()

    whole(WPR, got_w)

    def store(g):
        part = pl.ds(g * SUB, SUB)
        return pltpu.make_async_copy(stage.at[part], out_ref.at[part], sent.at[8])

    @pl.loop(0, halves)
    def _(h):
        with jax.named_scope('w5'):
            whole(MPR.at[h], got.at[h, 0])
            whole(XPR.at[h], got.at[h, 2])
        with jax.named_scope('two'):
            level_two(h)
        with jax.named_scope('last'):
            @pl.loop(0, share)
            def _(i):
                g = h * share + i
                c, j = g // inner, g % inner
                rows = tile(g)
                band = pl.ds(pl.multiple_of(j * SUB, SUB), SUB)
                for X in range(cx):
                    levels = []
                    for Y in range(cy):
                        k, q, r = X * cy + Y, X // 2 + 1, Y // 2 + 1
                        t = TT[q, r, rows, :]
                        outer = TT[q + 2 * (X % 2) - 1, r, rows, :] + TT[q, r + 2 * (Y % 2) - 1, rows, :]
                        outer = outer + TZ[(q - 1) * ey + r - 1, rows, :] + 3.0 * t
                        value = U1b[X + 1, Y + 1, rows, :] + t * (1.0 - jacobi_weight)
                        levels.append(value + W1[k] * (B1[k, rows, :] + 0.125 * outer))
                    for x in (2 * X, 2 * X + 1):
                        values = turn([S2[c, x, y, band, :] + levels[y // 2] for y in range(ny)])
                        for i in range(SUB):
                            stage[g * SUB + i, x * ny:(x + 1) * ny, :] = values[i]
                store(g).start()

    with jax.named_scope('sent'):
        whole(S2, sent.at[0])
        whole(FZS, sent.at[1])
        whole(X1S, sent.at[2])
        whole(Z1R, sent.at[3])
        whole(MPR, sent.at[4])
        whole(WPR, sent.at[5])
        whole(EPS, sent.at[6])
        whole(XPR, sent.at[7])
        whole(stage, sent.at[8])


def local(orbitals, potential, centre, half_width):
    bands, nx, ny, nz = orbitals.shape
    chunks = 4
    deep = bands // chunks
    cx, cy, ex, ey = nx // 2, ny // 2, nx // 4, ny // 4
    groups = bands // SUB
    vmem = lambda *s: pltpu.VMEM(s, jnp.float32)
    dma = lambda *s: pltpu.SemaphoreType.DMA(s)
    out = pl.pallas_call(
        functools.partial(kernel, bands, nx, ny, chunks),
        name="filter_orbitals",
        out_shape=jax.ShapeDtypeStruct((bands, nx * ny, nz), jnp.float32),
        in_specs=[pl.BlockSpec(memory_space=pltpu.HBM)] * 4,
        out_specs=pl.BlockSpec(memory_space=pl.ANY),
        scratch_shapes=[
            vmem(bands, nx * ny, nz), vmem(nx * ny, nz), pltpu.SMEM((bands,), jnp.float32), pltpu.SMEM((bands,), jnp.float32),
            vmem(nx * ny, bands, nz), vmem(cx * cy, deep, nz),
            vmem(chunks, nx + 2, ny + 2, deep, nz), vmem(chunks, nx + 2, ny + 2, deep, nz), vmem(chunks, nx, ny, deep, nz),
            vmem(nx * ny, SUB, nz), vmem(cx * cy, SUB, nz), vmem(cx * cy, SUB, nz),
            vmem(groups, SUB, nz), vmem(groups, SUB, nz),
            vmem(2, 2, chunks, deep // 16, SUB, nz), vmem(2, 2, chunks, deep // 16, SUB, nz),
            vmem(cx * cy, bands, nz),
            vmem(cx + 2, cy + 2, bands, nz), vmem(cx + 2, cy + 2, bands, nz), vmem(ex * ey, bands, nz),
            vmem(2, 4, cy // 2, bands, nz), vmem(2, 4, cy // 2, bands, nz),
            vmem(2, groups // 2, SUB, nz), vmem(2, 2, groups // 2, SUB, nz),
            vmem(2, groups // 2, SUB, nz), vmem(2, 10, groups // 2, SUB, nz), vmem(SUB, nz), vmem(10, SUB, nz),
            vmem(2, 2, SUB, nz), vmem(2, 2, SUB, nz), vmem(2, 8, 2, SUB, nz),
            vmem(9, groups // 2 + 1, SUB, nz), vmem(groups // 2, 14, SUB, nz), vmem(groups // 2, 14, SUB, nz),
            vmem(ex + 2, ey + 2, bands, nz), vmem(ex * ey, bands, nz),
            dma(chunks), dma(3), dma(9), dma(2, chunks, 2), dma(2, chunks, 2), dma(2, 3), pltpu.SemaphoreType.DMA,
        ],
        compiler_params=pltpu.CompilerParams(collective_id=0, has_side_effects=True, vmem_limit_bytes=48 * 1024 * 1024),
    )(*(pltpu.with_memory_space_constraint(a, pltpu.HBM) for a in (orbitals.reshape(bands, nx * ny, nz), potential.reshape(nx * ny, nz), centre, half_width)))
    return out.reshape(bands, nx, ny, nz)


def solution(mesh):
    in_specs = (P(None, "gx", "gy", "gz"), P("gx", "gy", "gz"), P(), P())
    out_specs = P(None, "gx", "gy", "gz")
    return jax.shard_map(local, mesh=mesh, in_specs=in_specs, out_specs=out_specs, check_vma=False)
```

time: 59.9 us -> 48.8 us (0.81)
  the two profiles are of different devices: /device:TPU:0 before, /device:TPU:1 now
where the time goes in v3:
time: 48.8 us; the launch traced here: 48.7 us
  Pallas kernels  47.3 us (97%)
  local copies, waits for them, and re-layouts  1.32 us (3%)
    pallas_call x1, Pallas kernels, local(): pl.pallas_call(functools.partial(kernel, bands, nx, ny, chunks), name='fi...  47.3 us
    unnamed x1, local copies, waits for them, and re-layouts  1.32 us

profile of v3, /device:TPU:1, one launch (start us, length us, event | category | flops | bytes accessed | tf_op | source)
XLA Modules:
  0.0 48.7 jit_solution(8384004551222285749)
XLA Ops:
  0.0 47.3 %filter_orbitals.1 = f32[64,64,128]{2,1,0:T(8,128)S(1)} custom-call(f32[64,64,128]{2,1,0:T(8,128)} %bitcast.4, f32[64,128]{1,0:T(8,128)} %bitcast.5, f32[64]{0:T(128)} %mid_hbm.1, f32[64]{0:T(128)} %half_hbm.1), custom_call_target="tpu_custom_call" | custom-call | tf_op jit(solution)/shard_map/filter_orbitals/pallas_call | solution.py:643
  47.3 1.3 %copy.6 = f32[64,8,8,128]{3,2,1,0:T(8,128)} copy(f32[64,8,8,128]{3,2,1,0:T(8,128)S(1)} %bitcast.3) | data formatting | bytes 4194304

commit v4 on v3

--- a/solution.py
+++ b/solution.py
@@ -120,6 +120,14 @@
             n = lax.axis_size(axis)
             place[axis] = lax.rem(lax.axis_index(axis) + (n + k), n)
         around_xy.append(place)
+    around_z = []
+    for step in NEAR:
+        for k in (1, -1):
+            place = {}
+            for axis, move in zip(AXES, step + (k,)):
+                n = lax.axis_size(axis)
+                place[axis] = lax.rem(lax.axis_index(axis) + (n + move), n)
+            around_z.append(place)
 
     def load(c):
         part = pl.ds(c * deep, deep)
@@ -132,7 +140,7 @@
     for c in range(chunks):
         load(c).start()
     barrier = pltpu.get_barrier_semaphore()
-    for peer in peers + around_xy[4:]:
+    for peer in peers:
         pl.semaphore_signal(barrier, inc=1, device_id=peer, device_id_type=MESH)
 
     def shape(value):
@@ -341,10 +349,12 @@
     def ends(h):
         return [send(EPS.at[h, d], EPR.at[h, d], sent.at[6], got.at[h, 1], 4 + d) for d in range(2)]
 
-    def forward(h):
+    def ends_far(h):
         copies = []
         for i, (a, b) in enumerate(NEAR):
-            copies.append(remote(EPR.at[h], XPR.at[h, slot((-a, -b))], sent.at[7], got.at[h, 2], around_xy[i]))
+            for d in range(2):
+                copies.append(remote(EPS.at[h, d], XPR.at[h, slot((-a, -b)), d], sent.at[7], got.at[h, 2],
+                                     around_z[2 * i + d]))
         return copies
 
     def tile(g):
@@ -480,10 +490,13 @@
             for q in range(ex * ey):
                 TZ[q, tile(h * share + g), :] = spread(PA[g, 0], PA[g, 1], q)
 
+    start_fine(0)
     with jax.named_scope('barrier'):
-        pl.semaphore_wait(barrier, 12)
-
-    @pl.loop(0, chunks)
+        pl.semaphore_wait(barrier, 6)
+    for copy in fine(A, 0, 0):
+        copy.start()
+
+    @pl.loop(1, chunks)
     def _(c):
         with jax.named_scope('load'):
             start_fine(c)
@@ -492,8 +505,6 @@
 
     with jax.named_scope('prologue'):
         prologue()
-    for copy in gather_diagonal():
-        copy.start()
 
     @pl.loop(0, chunks)
     def _(c):
@@ -512,6 +523,9 @@
             second_pass(c)
         for copy in one(0, c):
             copy.start()
+
+    for copy in gather_diagonal():
+        copy.start()
 
     @pl.loop(0, chunks)
     def _(c):
@@ -575,14 +589,7 @@
                 high = up if high is None else jnp.where(here, up, high)
                 low = down if low is None else jnp.where(here, down, low)
             EPS[h, 0], EPS[h, 1] = high, low
-        for copy in ends(h) + gather(h):
-            copy.start()
-
-    @pl.loop(0, halves)
-    def _(h):
-        with jax.named_scope('w4'):
-            whole(EPR.at[h], got.at[h, 1])
-        for copy in forward(h):
+        for copy in ends_far(h) + ends(h) + gather(h):
             copy.start()
 
     whole(WPR, got_w)
@@ -595,6 +602,8 @@
     def _(h):
         with jax.named_scope('w5'):
             whole(MPR.at[h], got.at[h, 0])
+        with jax.named_scope('w6'):
+            whole(EPR.at[h], got.at[h, 1])
             whole(XPR.at[h], got.at[h, 2])
         with jax.named_scope('two'):
             level_two(h)

time: 48.8 us -> 45.9 us (0.941)
  Pallas kernels: 47.3 us -> 44.5 us
    pallas_call x1, Pallas kernels: 47.3 us -> 44.5 us  [local(): pl.pallas_call(functools.partial(kernel, bands, nx, ny, chunks), name='fi...]
where the time goes in v4:
time: 45.9 us; the launch traced here: 45.8 us
  Pallas kernels  44.5 us (97%)
  local copies, waits for them, and re-layouts  1.32 us (3%)
    pallas_call x1, Pallas kernels, local(): pl.pallas_call(functools.partial(kernel, bands, nx, ny, chunks), name='fi...  44.5 us
    unnamed x1, local copies, waits for them, and re-layouts  1.32 us

profile of v4, /device:TPU:1, one launch (start us, length us, event | category | flops | bytes accessed | tf_op | source)
XLA Modules:
  0.0 45.8 jit_solution(300886127737360962)
XLA Ops:
  0.0 44.5 %filter_orbitals.1 = f32[64,64,128]{2,1,0:T(8,128)S(1)} custom-call(f32[64,64,128]{2,1,0:T(8,128)} %bitcast.4, f32[64,128]{1,0:T(8,128)} %bitcast.5, f32[64]{0:T(128)} %mid_hbm.1, f32[64]{0:T(128)} %half_hbm.1), custom_call_target="tpu_custom_call" | custom-call | tf_op jit(solution)/shard_map/filter_orbitals/pallas_call | solution.py:652
  44.5 1.3 %copy.6 = f32[64,8,8,128]{3,2,1,0:T(8,128)} copy(f32[64,8,8,128]{3,2,1,0:T(8,128)S(1)} %bitcast.3) | data formatting | bytes 4194304

commit v5 on v4

--- a/solution.py
+++ b/solution.py
@@ -16,6 +16,7 @@
 RING = ((1, 0), (-1, 0), (0, 1), (0, -1), (1, 1), (1, -1), (-1, 1), (-1, -1), (2, 0), (0, 2))
 NEAR = RING[:8]
 CROSS = RING[:4]
+CORNERS = RING[4:8]
 EDGE = 16
 
 
@@ -100,8 +101,9 @@
 
 def kernel(bands, nx, ny, chunks, orb_hbm, pot_hbm, mid_hbm, half_hbm, out_ref,
            stage, pot_ref, mid_ref, half_ref, ZS, TS, A, F, S2, DG, D1, W1, MID, INV, FZS, FZR,
-           B1, U1a, U1b, B2, X1S, X1R, Z1S, Z1R, MPS, MPR, WPS, WPR, EPS, EPR, XPR, XE, PA, PB, TT, TZ,
+           B1, U1a, U1b, B2, X1S, X1R, Z1S, Z1R, CS, CR, ZD, W1R, WZS, WZR, HU, ZRING, MPS, MPR, WPS, WPR, EPS, EPR, XPR, XE, PA, PB, TT, TZ,
            in_sem, par_sem, sent, fine_got, one_got, got, got_w):
+    third = 1.0 - jacobi_weight
     deep = bands // chunks
     inner = deep // SUB
     groups = bands // SUB
@@ -172,7 +174,7 @@
                 ones[X, Y] = one
                 diagonal = 0.75 + one + shift_mass
                 D1[X * cy + Y] = diagonal
-                W1[X * cy + Y] = jacobi_weight / diagonal
+                W1[X, Y] = jacobi_weight / diagonal
         two_diagonals = []
         for X in range(ex):
             for Y in range(ey):
@@ -180,6 +182,11 @@
                 diagonal = 0.1875 + 0.125 * pair_sum(total, 2) + shift_mass
                 two_diagonals.append(jacobi_weight / diagonal)
         WPS[...] = woven(two_diagonals)
+        total = None
+        for j in range(2):
+            for k in range(cx * cy):
+                total = packed(total, W1[k // cy, k % cy], 4 * (j * cx * cy + k), 4)
+        WZS[...] = total
 
     def send(src, dst, s, r, d):
         return pltpu.make_async_remote_copy(
@@ -263,25 +270,6 @@
                 for y in range(ny):
                     totals[j] = packed(totals[j], F[c, x + 1, y + 1, j * SUB:(j + 1) * SUB, :], 2 * (x * ny + y), 2)
         fine_edges(1, c, totals)
-
-    def faces(buffer, n, m, tile, count):
-        even = (lane() & 1) == 0
-        rows = pl.ds(tile, SUB)
-        lines = ([(n, y) for y in range(1, m + 1)], [(1, y) for y in range(1, m + 1)],
-                 [(x, m) for x in range(1, n + 1)], [(x, 1) for x in range(1, n + 1)])
-        return [[jnp.where(even, buffer[l[2 * p][0], l[2 * p][1], rows, :], buffer[l[2 * p + 1][0], l[2 * p + 1][1], rows, :])
-                 for p in range(count)] for l in lines]
-
-    def unfaces(buffer, received, rnd, n, m, count, g):
-        even = (lane() & 1) == 0
-        rows = tile(g)
-        lines = ([(0, y) for y in range(1, m + 1)], [(n + 1, y) for y in range(1, m + 1)],
-                 [(x, 0) for x in range(1, n + 1)], [(x, m + 1) for x in range(1, n + 1)])
-        for d, l in enumerate(lines):
-            for p in range(count):
-                both = received[rnd, d, p, rows, :]
-                buffer[l[2 * p][0], l[2 * p][1], rows, :] = jnp.where(even, both, roll(both, 1))
-                buffer[l[2 * p + 1][0], l[2 * p + 1][1], rows, :] = jnp.where(even, roll(both, -1), both)
 
     def second_pass(c):
         fine_z(F, 1, c)
@@ -301,31 +289,53 @@
                             total = value if total is None else total + value
                     TS[X * cy + Y, band, :] = total
 
-        zs = None
+        totals = [None, None]
         for j in range(inner):
             rows = pl.ds(pl.multiple_of(c * deep + j * SUB, SUB), SUB)
             for X in range(cx):
                 for Y in range(cy):
-                    source = 0.5 * pair_sum(TS[X * cy + Y, j * SUB:(j + 1) * SUB, :], 1)
-                    B1[X * cy + Y, rows, :] = source
-                    level = W1[X * cy + Y] * source
-                    U1a[X + 1, Y + 1, rows, :] = level
-                    zs = packed(zs, level, j * 64 + 4 * (X * cy + Y), 4)
-            for d, line in enumerate(faces(U1a, cx, cy, c * deep + j * SUB, cy // 2)):
-                for p, value in enumerate(line):
-                    X1S[0, d, p, rows, :] = value
-        Z1S[0, c] = zs
-
-    def one(rnd, c):
+                    k = X * cy + Y
+                    source = 0.5 * pair_sum(TS[k, j * SUB:(j + 1) * SUB, :], 1)
+                    B1[k, rows, :] = source
+                    level = W1[X, Y] * source
+                    U1a[X + 2, Y + 2, rows, :] = level
+                    start = 4 * (j * cx * cy + k)
+                    moved = roll(level, start + 2)
+                    here = ((lane() + (LANES - start + 2)) & (LANES - 1)) < 8
+                    totals[k % 2] = moved if totals[k % 2] is None else jnp.where(here, moved, totals[k % 2])
+            even = (lane() & 1) == 0
+            for n in range(2):
+                lines = ([(cx - 1 - n, y) for y in range(cy)], [(n, y) for y in range(cy)],
+                         [(x, cy - 1 - n) for x in range(cx)], [(x, n) for x in range(cx)])
+                for d, line in enumerate(lines):
+                    for p in range(len(line) // 2):
+                        (x0, y0), (x1, y1) = line[2 * p], line[2 * p + 1]
+                        X1S[n, d, p, rows, :] = jnp.where(even, U1a[x0 + 2, y0 + 2, rows, :], U1a[x1 + 2, y1 + 2, rows, :])
+        turn_even = (lane() & 4) == 0
+        Z1S[c, 0] = jnp.where(turn_even, totals[0], totals[1])
+        inward = [jnp.where((lane() & 2) == 0, roll(t, 2), roll(t, -2)) for t in totals]
+        Z1S[c, 1] = jnp.where(turn_even, inward[0], inward[1])
+        for i, (a, b) in enumerate(CORNERS):
+            x, y = cx + 1 if a > 0 else 2, cy + 1 if b > 0 else 2
+            CS[i, c] = jnp.where((lane() & 1) == 0, U1a[x, y, tile(c * inner), :], U1a[x, y, tile(c * inner + 1), :])
+
+    def one(c):
         rows = pl.ds(pl.multiple_of(c * deep, deep), deep)
-        copies = [send(X1S.at[rnd, d, :, rows], X1R.at[rnd, d, :, rows], sent.at[2], one_got.at[rnd, c, 0], d)
-                  for d in range(4)]
-        return copies + [send(Z1S.at[rnd, c], Z1R.at[rnd, d - 4, c], sent.at[3], one_got.at[rnd, c, 1], d) for d in (4, 5)]
-
-    def one_wait(rnd, c):
-        rows = pl.ds(pl.multiple_of(c * deep, deep), deep)
-        whole(X1R.at[rnd, :, :, rows], one_got.at[rnd, c, 0])
-        whole(Z1R.at[rnd, :, c], one_got.at[rnd, c, 1])
+        copies = []
+        for i, (a, b) in enumerate(CROSS):
+            for d in range(2):
+                copies.append(remote(Z1S.at[c, 0], ZD.at[slot((-a, -b)), d, c], sent.at[10], one_got.at[c, 3],
+                                     around_z[2 * i + d]))
+        copies += [send(Z1S.at[c], Z1R.at[d - 4, c], sent.at[3], one_got.at[c, 1], d) for d in (4, 5)]
+        for i in range(4):
+            copies.append(remote(CS.at[i, c], CR.at[i, c], sent.at[9], one_got.at[c, 2], around_xy[4 + i]))
+        return copies + [send(X1S.at[:, d, :, rows], X1R.at[:, d, :, rows], sent.at[2], one_got.at[c, 0], d)
+                         for d in range(4)]
+
+    def diagonals():
+        faces = (W1.at[cx - 1], W1.at[0], W1.at[:, cy - 1], W1.at[:, 0])
+        copies = [send(face, W1R.at[d ^ 1], sent.at[11], got_w.at[1], d) for d, face in enumerate(faces)]
+        return copies + [send(WZS, WZR.at[d - 4], sent.at[12], got_w.at[2], d) for d in (4, 5)]
 
     def slot(step):
         return RING.index(step) if step in RING else RING.index((abs(step[0]), abs(step[1])))
@@ -343,7 +353,7 @@
     def gather_diagonal():
         copies = []
         for i, (a, b) in enumerate(RING):
-            copies.append(remote(WPS, WPR.at[slot((-a, -b))], sent.at[5], got_w, around_xy[i]))
+            copies.append(remote(WPS, WPR.at[slot((-a, -b))], sent.at[5], got_w.at[0], around_xy[i]))
         return copies
 
     def ends(h):
@@ -360,39 +370,54 @@
     def tile(g):
         return pl.ds(g * SUB if isinstance(g, int) else pl.multiple_of(g * SUB, SUB), SUB)
 
-    def coarse_z(buffer, rnd, c):
-        rims = met(Z1R[rnd, 0, c], Z1R[rnd, 1, c], 4)
+    def coarse_z(buffer, at, rims, c):
         for j in range(inner):
             for X in range(cx):
                 for Y in range(cy):
                     k = X * cy + Y
-                    value = buffer[X + 1, Y + 1, tile(c * inner + j), :]
+                    value = buffer[X + at, Y + at, tile(c * inner + j), :]
                     ZS[k, tile(c * inner + j), :] = along_z(value, rims, 4 * (j * cx * cy + k), 4)
 
-    def coarse_edges(buffer, rnd, c):
-        zs = None
+    def unpack_faces(c):
+        even = (lane() & 1) == 0
         for j in range(inner):
-            for X in range(cx):
-                for Y in range(cy):
-                    zs = packed(zs, buffer[X + 1, Y + 1, tile(c * inner + j), :], 4 * (j * cx * cy + X * cy + Y), 4)
-        Z1S[rnd, c] = zs
-
-    def around(buffer, X, Y, m, g):
-        rows = tile(g)
-        u = buffer[X + 1, Y + 1, rows, :]
-        total = buffer[X, Y + 1, rows, :] + buffer[X + 2, Y + 1, rows, :]
-        total = total + buffer[X + 1, Y, rows, :] + buffer[X + 1, Y + 2, rows, :]
-        return u, total + ZS[X * m + Y, rows, :]
-
-    def send_faces(buffer, out, rnd, n, m, g):
-        rows = tile(g)
-        for d, line in enumerate(faces(buffer, n, m, rows.start, m // 2)):
-            for p, value in enumerate(line):
-                out[rnd, d, p, rows, :] = value
-
-    def sweep_one(buffer, g, X, Y):
-        u, total = around(buffer, X, Y, cy, g)
-        return u * (1.0 - jacobi_weight) + W1[X * cy + Y] * (B1[X * cy + Y, tile(g), :] + 0.125 * total)
+            rows = tile(c * inner + j)
+            for n in range(2):
+                lines = ([(1 - n, y + 2) for y in range(cy)], [(cx + 2 + n, y + 2) for y in range(cy)],
+                         [(x + 2, 1 - n) for x in range(cx)], [(x + 2, cy + 2 + n) for x in range(cx)])
+                for d, line in enumerate(lines):
+                    for p in range(len(line) // 2):
+                        both = X1R[n, d, p, rows, :]
+                        (x0, y0), (x1, y1) = line[2 * p], line[2 * p + 1]
+                        U1a[x0, y0, rows, :] = jnp.where(even, both, roll(both, 1))
+                        U1a[x1, y1, rows, :] = jnp.where(even, roll(both, -1), both)
+        for i, (a, b) in enumerate(CORNERS):
+            both = CR[i, c]
+            x, y = 1 if a > 0 else cx + 2, 1 if b > 0 else cy + 2
+            U1a[x, y, tile(c * inner), :] = jnp.where(even, both, roll(both, 1))
+            U1a[x, y, tile(c * inner + 1), :] = jnp.where(even, roll(both, -1), both)
+
+    def ring(i, t):
+        return (((cx, t), t), ((-1, t), (cx - 1) * cy + t), ((t, cy), t * cy), ((t, -1), t * cy + cy - 1))[i]
+
+    def outside(c):
+        rims = [met(ZD[i, 0, c], ZD[i, 1, c], 4) for i in range(4)]
+        for j in range(inner):
+            for i in range(4):
+                for t in range(4):
+                    (x, y), k = ring(i, t)
+                    value = U1a[x + 2, y + 2, tile(c * inner + j), :]
+                    ZRING[4 * i + t, j * SUB:(j + 1) * SUB, :] = along_z(value, rims[i], 4 * (j * cx * cy + k), 4)
+        own = met(Z1R[0, c, 0], Z1R[1, c, 0], 4)
+        X, Y = (lane() >> 4) & 3, (lane() >> 2) & 3
+        total = jnp.where(X == 0, roll(rims[1], -48), roll(own, 16)) + jnp.where(X == 3, roll(rims[0], 48), roll(own, -16))
+        total = total + jnp.where(Y == 0, roll(rims[3], -12), roll(own, 4)) + jnp.where(Y == 3, roll(rims[2], 12), roll(own, -4))
+        total = total + Z1S[c, 0] + met(Z1R[0, c, 1], Z1R[1, c, 1], 4)
+        HU[c] = own * (1.0 + third) + 0.125 * met(WZR[0], WZR[1], 4) * total
+
+    def beside_xy(buffer, x, y, rows):
+        total = buffer[x - 1, y, rows, :] + buffer[x + 1, y, rows, :]
+        return total + buffer[x, y - 1, rows, :] + buffer[x, y + 1, rows, :]
 
     def level_two(h):
         at = lane()
@@ -505,6 +530,8 @@
 
     with jax.named_scope('prologue'):
         prologue()
+    for copy in diagonals():
+        copy.start()
 
     @pl.loop(0, chunks)
     def _(c):
@@ -521,59 +548,71 @@
             fine_wait(1, c)
         with jax.named_scope('second'):
             second_pass(c)
-        for copy in one(0, c):
+        for copy in one(c):
             copy.start()
 
     for copy in gather_diagonal():
         copy.start()
 
-    @pl.loop(0, chunks)
-    def _(c):
-        with jax.named_scope('w2'):
-            one_wait(0, c)
-        with jax.named_scope('sweep'):
-            for j in range(inner):
-                unfaces(U1a, X1R, 0, cx, cy, cy // 2, c * inner + j)
-            coarse_z(U1a, 0, c)
-
-            @pl.loop(0, inner)
-            def _(j):
-                g = c * inner + j
-                for X in range(cx):
-                    for Y in range(cy):
-                        U1b[X + 1, Y + 1, tile(g), :] = sweep_one(U1a, g, X, Y)
-                send_faces(U1b, X1S, 1, cx, cy, g)
-
-            coarse_edges(U1b, 1, c)
-        for copy in one(1, c):
-            copy.start()
+    whole(W1R, got_w.at[1])
+    whole(WZR, got_w.at[2])
 
     @pl.loop(0, halves)
     def _(h):
         @pl.loop(0, chunks // halves)
         def _(i):
             c = h * (chunks // halves) + i
-            with jax.named_scope('w3'):
-                one_wait(1, c)
-            with jax.named_scope('residue'):
-                for j in range(inner):
-                    unfaces(U1b, X1R, 1, cx, cy, cy // 2, c * inner + j)
-                coarse_z(U1b, 1, c)
+            with jax.named_scope('w2'):
+                whole(X1R.at[:, :, :, pl.ds(pl.multiple_of(c * deep, deep), deep)], one_got.at[c, 0])
+                whole(Z1R.at[:, c], one_got.at[c, 1])
+                whole(CR.at[:, c], one_got.at[c, 2])
+            with jax.named_scope('sweep'):
+                unpack_faces(c)
+                coarse_z(U1a, 2, met(Z1R[0, c, 0], Z1R[1, c, 0], 4), c)
 
                 @pl.loop(0, inner)
                 def _(j):
-                    g = c * inner + j
+                    rows = tile(c * inner + j)
+                    for X in range(cx):
+                        for Y in range(cy):
+                            k = X * cy + Y
+                            total = beside_xy(U1a, X + 2, Y + 2, rows) + ZS[k, rows, :]
+                            value = U1a[X + 2, Y + 2, rows, :] * third
+                            U1b[X + 1, Y + 1, rows, :] = value + W1[X, Y] * (B1[k, rows, :] + 0.125 * total)
+
+            with jax.named_scope('w3'):
+                whole(ZD.at[:, :, c], one_got.at[c, 3])
+            with jax.named_scope('ring'):
+                outside(c)
+
+                @pl.loop(0, inner)
+                def _(j):
+                    rows = tile(c * inner + j)
+                    for side in range(4):
+                        for t in range(4):
+                            (x, y), _k = ring(side, t)
+                            total = beside_xy(U1a, x + 2, y + 2, rows) + ZRING[4 * side + t, pl.ds(pl.multiple_of(j * SUB, SUB), SUB), :]
+                            value = U1a[x + 2, y + 2, rows, :] * (1.0 + third)
+                            U1b[x + 1, y + 1, rows, :] = value + 0.125 * W1R[side, t] * total
+
+            with jax.named_scope('residue'):
+                coarse_z(U1b, 1, HU[c], c)
+
+                @pl.loop(0, inner)
+                def _(j):
+                    rows = tile(c * inner + j)
                     for X in range(ex):
                         for Y in range(ey):
                             sums = None
                             for dx in range(2):
                                 for dy in range(2):
                                     x, y = 2 * X + dx, 2 * Y + dy
-                                    u, total = around(U1b, x, y, cy, g)
-                                    residue = B1[x * cy + y, tile(g), :] - D1[x * cy + y] * u + 0.125 * total
-                                    B1[x * cy + y, tile(g), :] = residue
+                                    k = x * cy + y
+                                    total = beside_xy(U1b, x + 1, y + 1, rows) + ZS[k, rows, :]
+                                    residue = B1[k, rows, :] - D1[k] * U1b[x + 1, y + 1, rows, :] + 0.125 * total
+                                    B1[k, rows, :] = residue
                                     sums = residue if sums is None else sums + residue
-                            B2[X * ey + Y, tile(g), :] = sums
+                            B2[X * ey + Y, rows, :] = sums
 
         with jax.named_scope('weave'):
             parts = []
@@ -592,7 +631,7 @@
         for copy in ends_far(h) + ends(h) + gather(h):
             copy.start()
 
-    whole(WPR, got_w)
+    whole(WPR, got_w.at[0])
 
     def store(g):
         part = pl.ds(g * SUB, SUB)
@@ -622,7 +661,7 @@
                         outer = TT[q + 2 * (X % 2) - 1, r, rows, :] + TT[q, r + 2 * (Y % 2) - 1, rows, :]
                         outer = outer + TZ[(q - 1) * ey + r - 1, rows, :] + 3.0 * t
                         value = U1b[X + 1, Y + 1, rows, :] + t * (1.0 - jacobi_weight)
-                        levels.append(value + W1[k] * (B1[k, rows, :] + 0.125 * outer))
+                        levels.append(value + W1[X, Y] * (B1[k, rows, :] + 0.125 * outer))
                     for x in (2 * X, 2 * X + 1):
                         values = turn([S2[c, x, y, band, :] + levels[y // 2] for y in range(ny)])
                         for i in range(SUB):
@@ -639,6 +678,10 @@
         whole(EPS, sent.at[6])
         whole(XPR, sent.at[7])
         whole(stage, sent.at[8])
+        whole(CS, sent.at[9])
+        whole(ZD, sent.at[10])
+        whole(W1R, sent.at[11])
+        whole(WZR, sent.at[12])
 
 
 def local(orbitals, potential, centre, half_width):
@@ -659,18 +702,20 @@
             vmem(bands, nx * ny, nz), vmem(nx * ny, nz), pltpu.SMEM((bands,), jnp.float32), pltpu.SMEM((bands,), jnp.float32),
             vmem(nx * ny, bands, nz), vmem(cx * cy, deep, nz),
             vmem(chunks, nx + 2, ny + 2, deep, nz), vmem(chunks, nx + 2, ny + 2, deep, nz), vmem(chunks, nx, ny, deep, nz),
-            vmem(nx * ny, SUB, nz), vmem(cx * cy, SUB, nz), vmem(cx * cy, SUB, nz),
+            vmem(nx * ny, SUB, nz), vmem(cx * cy, SUB, nz), vmem(cx, cy, SUB, nz),
             vmem(groups, SUB, nz), vmem(groups, SUB, nz),
             vmem(2, 2, chunks, deep // 16, SUB, nz), vmem(2, 2, chunks, deep // 16, SUB, nz),
             vmem(cx * cy, bands, nz),
-            vmem(cx + 2, cy + 2, bands, nz), vmem(cx + 2, cy + 2, bands, nz), vmem(ex * ey, bands, nz),
+            vmem(cx + 4, cy + 4, bands, nz), vmem(cx + 2, cy + 2, bands, nz), vmem(ex * ey, bands, nz),
             vmem(2, 4, cy // 2, bands, nz), vmem(2, 4, cy // 2, bands, nz),
-            vmem(2, groups // 2, SUB, nz), vmem(2, 2, groups // 2, SUB, nz),
+            vmem(chunks, 2, SUB, nz), vmem(2, chunks, 2, SUB, nz),
+            vmem(4, chunks, SUB, nz), vmem(4, chunks, SUB, nz), vmem(4, 2, chunks, SUB, nz),
+            vmem(4, 4, SUB, nz), vmem(SUB, nz), vmem(2, SUB, nz), vmem(chunks, SUB, nz), vmem(16, deep, nz),
             vmem(2, groups // 2, SUB, nz), vmem(2, 10, groups // 2, SUB, nz), vmem(SUB, nz), vmem(10, SUB, nz),
             vmem(2, 2, SUB, nz), vmem(2, 2, SUB, nz), vmem(2, 8, 2, SUB, nz),
             vmem(9, groups // 2 + 1, SUB, nz), vmem(groups // 2, 14, SUB, nz), vmem(groups // 2, 14, SUB, nz),
             vmem(ex + 2, ey + 2, bands, nz), vmem(ex * ey, bands, nz),
-            dma(chunks), dma(3), dma(9), dma(2, chunks, 2), dma(2, chunks, 2), dma(2, 3), pltpu.SemaphoreType.DMA,
+            dma(chunks), dma(3), dma(13), dma(2, chunks, 2), dma(chunks, 4), dma(2, 3), dma(3),
         ],
         compiler_params=pltpu.CompilerParams(collective_id=0, has_side_effects=True, vmem_limit_bytes=48 * 1024 * 1024),
     )(*(pltpu.with_memory_space_constraint(a, pltpu.HBM) for a in (orbitals.reshape(bands, nx * ny, nz), potential.reshape(nx * ny, nz), centre, half_width)))

time: 45.9 us -> 42.8 us (0.932)
  Pallas kernels: 44.5 us -> 41.4 us
    pallas_call x1, Pallas kernels: 44.5 us -> 41.4 us  [local(): pl.pallas_call(functools.partial(kernel, bands, nx, ny, chunks), name='fi...]
where the time goes in v5:
time: 42.8 us; the launch traced here: 42.7 us
  Pallas kernels  41.4 us (97%)
  local copies, waits for them, and re-layouts  1.32 us (3%)
    pallas_call x1, Pallas kernels, local(): pl.pallas_call(functools.partial(kernel, bands, nx, ny, chunks), name='fi...  41.4 us
    unnamed x1, local copies, waits for them, and re-layouts  1.32 us

profile of v5, /device:TPU:1, one launch (start us, length us, event | category | flops | bytes accessed | tf_op | source)
XLA Modules:
  0.0 42.7 jit_solution(576883927037527848)
XLA Ops:
  0.0 41.4 %filter_orbitals.1 = f32[64,64,128]{2,1,0:T(8,128)S(1)} custom-call(f32[64,64,128]{2,1,0:T(8,128)} %bitcast.4, f32[64,128]{1,0:T(8,128)} %bitcast.5, f32[64]{0:T(128)} %mid_hbm.1, f32[64]{0:T(128)} %half_hbm.1), custom_call_target="tpu_custom_call" | custom-call | tf_op jit(solution)/shard_map/filter_orbitals/pallas_call | solution.py:695
  41.4 1.3 %copy.6 = f32[64,8,8,128]{3,2,1,0:T(8,128)} copy(f32[64,8,8,128]{3,2,1,0:T(8,128)S(1)} %bitcast.3) | data formatting | bytes 4194304

commit v6 on v5

--- a/solution.py
+++ b/solution.py
@@ -66,11 +66,11 @@
 
 
 def below(main, other):
-    return jnp.where(lane() < 4, roll(other, 4), roll(main, 4))
+    return roll(jnp.where(lane() >= LANES - 4, other, main), 4)
 
 
 def above(main, other):
-    return jnp.where(lane() >= LANES - 4, roll(other, -4), roll(main, -4))
+    return roll(jnp.where(lane() < 4, other, main), -4)
 
 
 def packed(total, value, start, width):
@@ -81,12 +81,14 @@
     return jnp.where((at >= start) & (at < start + width), moved, total)
 
 
-def along_z(value, rims, start, width):
+def inner_z(value, width):
     at, half = lane(), width // 2
-    outer = roll(rims, -(start + half))
-    left = jnp.where(at < half, outer, roll(value, half))
-    right = jnp.where(at >= LANES - half, outer, roll(value, -half))
-    return left + right
+    return jnp.where(at < half, 0.0, roll(value, half)) + jnp.where(at >= LANES - half, 0.0, roll(value, -half))
+
+
+def outer_z(rims, start, width):
+    half = width // 2
+    return jnp.where(((lane() + half) & (LANES - 1)) < width, roll(rims, -(start + half)), 0.0)
 
 
 def met(from_left, from_right, width):
@@ -94,6 +96,10 @@
     return jnp.where((lane() & half) != 0, roll(from_left, half), roll(from_right, -half))
 
 
+def first_cells(from_left, from_right):
+    return jnp.where((lane() & 2) == 0, from_right, roll(from_left, 2))
+
+
 def pair_sum(value, cell):
     at = lane()
     return value + jnp.where((at & cell) == 0, roll(value, -cell), roll(value, cell))
@@ -101,7 +107,7 @@
 
 def kernel(bands, nx, ny, chunks, orb_hbm, pot_hbm, mid_hbm, half_hbm, out_ref,
            stage, pot_ref, mid_ref, half_ref, ZS, TS, A, F, S2, DG, D1, W1, MID, INV, FZS, FZR,
-           B1, U1a, U1b, B2, X1S, X1R, Z1S, Z1R, CS, CR, ZD, W1R, WZS, WZR, HU, ZRING, MPS, MPR, WPS, WPR, EPS, EPR, XPR, XE, PA, PB, TT, TZ,
+           B1, U1a, U1b, B2, X1S, X1R, Z1S, Z1R, CS, CR, ZD, ENDS, W1R, WZS, WZR, HU, ZRING, MPS, MPR, WPS, WPR, EPS, EPR, XPR, XE, PA, PB, TT, TZ,
            in_sem, par_sem, sent, fine_got, one_got, got, got_w):
     third = 1.0 - jacobi_weight
     deep = bands // chunks
@@ -201,14 +207,13 @@
             (FZS.at[rnd, 0, c], FZR.at[rnd, 0, c]),
             (FZS.at[rnd, 1, c], FZR.at[rnd, 1, c]),
         )
-        return [send(a, b, sent.at[d // 4], fine_got.at[rnd, c, d // 4], d) for d, (a, b) in enumerate(ends)]
+        return [send(a, b, sent.at[d // 4], fine_got.at[rnd, c], d) for d, (a, b) in enumerate(ends)]
 
     def whole(ref, sem):
         pltpu.make_async_copy(ref, ref, sem).wait()
 
     def fine_wait(rnd, c):
-        whole(stage.at[pl.ds(0, 2 * deep * (nx + ny) // (nx * ny))], fine_got.at[rnd, c, 0])
-        whole(FZR.at[rnd, :, c], fine_got.at[rnd, c, 1])
+        whole(stage.at[pl.ds(0, 2 * (nx + ny) + 1), pl.ds(0, deep)], fine_got.at[rnd, c])
 
     def fine_edges(rnd, c, totals):
         odd = (lane() & 1) != 0
@@ -237,25 +242,29 @@
                     totals[j] = packed(totals[j], rows[y], 2 * (x * ny + y), 2)
         fine_edges(0, c, totals)
 
-    def fine_z(buffer, rnd, c):
-        rims = fine_rims(rnd, c)
-        for j in range(inner):
-            band = slice(j * SUB, (j + 1) * SUB)
+    def fine_inner(buffer, c):
+        for j in range(inner):
             for x in range(nx):
                 for y in range(ny):
-                    k = x * ny + y
-                    ZS[k, band, :] = along_z(buffer[c, x + 1, y + 1, band, :], rims[j], 2 * k, 2)
+                    value = buffer[c, x + 1, y + 1, j * SUB:(j + 1) * SUB, :]
+                    ZS[x * ny + y, tile(c * inner + j), :] = inner_z(value, 2)
+
+    def fine_outer(rnd, c):
+        rims = fine_rims(rnd, c)
+        for j in range(inner):
+            for k in range(nx * ny):
+                ZS[k, tile(c * inner + j), :] += outer_z(rims[j], 2 * k, 2)
 
     def apply(buffer, c, x, y, j):
         band = pl.ds(pl.multiple_of(j * SUB, SUB), SUB)
         v = buffer[c, x + 1, y + 1, band, :]
         total = buffer[c, x, y + 1, band, :] + buffer[c, x + 2, y + 1, band, :]
         total = total + buffer[c, x + 1, y, band, :] + buffer[c, x + 1, y + 2, band, :]
-        total = total + ZS[x * ny + y, band, :]
+        total = total + ZS[x * ny + y, tile(c * inner + j), :]
         return (DG[x * ny + y] + MID[c * inner + j]) * v - total
 
     def first_pass(c):
-        fine_z(A, 0, c)
+        fine_outer(0, c)
 
         @pl.loop(0, inner)
         def _(j):
@@ -272,7 +281,7 @@
         fine_edges(1, c, totals)
 
     def second_pass(c):
-        fine_z(F, 1, c)
+        fine_outer(1, c)
 
         @pl.loop(0, inner)
         def _(j):
@@ -312,9 +321,12 @@
                         (x0, y0), (x1, y1) = line[2 * p], line[2 * p + 1]
                         X1S[n, d, p, rows, :] = jnp.where(even, U1a[x0 + 2, y0 + 2, rows, :], U1a[x1 + 2, y1 + 2, rows, :])
         turn_even = (lane() & 4) == 0
-        Z1S[c, 0] = jnp.where(turn_even, totals[0], totals[1])
+        near = jnp.where(turn_even, totals[0], totals[1])
+        ENDS[c] = near
         inward = [jnp.where((lane() & 2) == 0, roll(t, 2), roll(t, -2)) for t in totals]
-        Z1S[c, 1] = jnp.where(turn_even, inward[0], inward[1])
+        far = jnp.where(turn_even, inward[0], inward[1])
+        Z1S[c, 0] = jnp.where((lane() & 2) == 0, near, roll(far, 2))
+        Z1S[c, 1] = jnp.where((lane() & 2) == 0, roll(near, -2), far)
         for i, (a, b) in enumerate(CORNERS):
             x, y = cx + 1 if a > 0 else 2, cy + 1 if b > 0 else 2
             CS[i, c] = jnp.where((lane() & 1) == 0, U1a[x, y, tile(c * inner), :], U1a[x, y, tile(c * inner + 1), :])
@@ -324,11 +336,11 @@
         copies = []
         for i, (a, b) in enumerate(CROSS):
             for d in range(2):
-                copies.append(remote(Z1S.at[c, 0], ZD.at[slot((-a, -b)), d, c], sent.at[10], one_got.at[c, 3],
+                copies.append(remote(Z1S.at[c, d], ZD.at[slot((-a, -b)), d, c], sent.at[10], one_got.at[c, 1],
                                      around_z[2 * i + d]))
-        copies += [send(Z1S.at[c], Z1R.at[d - 4, c], sent.at[3], one_got.at[c, 1], d) for d in (4, 5)]
+        copies += [send(Z1S.at[c, d - 4], Z1R.at[d - 4, c], sent.at[3], one_got.at[c, 0], d) for d in (4, 5)]
         for i in range(4):
-            copies.append(remote(CS.at[i, c], CR.at[i, c], sent.at[9], one_got.at[c, 2], around_xy[4 + i]))
+            copies.append(remote(CS.at[i, c], CR.at[i, c], sent.at[9], one_got.at[c, 0], around_xy[4 + i]))
         return copies + [send(X1S.at[:, d, :, rows], X1R.at[:, d, :, rows], sent.at[2], one_got.at[c, 0], d)
                          for d in range(4)]
 
@@ -370,13 +382,24 @@
     def tile(g):
         return pl.ds(g * SUB if isinstance(g, int) else pl.multiple_of(g * SUB, SUB), SUB)
 
-    def coarse_z(buffer, at, rims, c):
+    def coarse_inner(buffer, at, c):
         for j in range(inner):
             for X in range(cx):
                 for Y in range(cy):
-                    k = X * cy + Y
-                    value = buffer[X + at, Y + at, tile(c * inner + j), :]
-                    ZS[k, tile(c * inner + j), :] = along_z(value, rims, 4 * (j * cx * cy + k), 4)
+                    ZS[X * cy + Y, tile(c * inner + j), :] = inner_z(buffer[X + at, Y + at, tile(c * inner + j), :], 4)
+
+    def coarse_outer(rims, c):
+        for j in range(inner):
+            for k in range(cx * cy):
+                ZS[k, tile(c * inner + j), :] += outer_z(rims, 4 * (j * cx * cy + k), 4)
+
+    def ring_inner(c):
+        for j in range(inner):
+            for i in range(4):
+                for t in range(4):
+                    (x, y), _ = ring(i, t)
+                    value = U1a[x + 2, y + 2, tile(c * inner + j), :]
+                    ZRING[4 * i + t, j * SUB:(j + 1) * SUB, :] = inner_z(value, 4)
 
     def unpack_faces(c):
         even = (lane() & 1) == 0
@@ -401,18 +424,18 @@
         return (((cx, t), t), ((-1, t), (cx - 1) * cy + t), ((t, cy), t * cy), ((t, -1), t * cy + cy - 1))[i]
 
     def outside(c):
-        rims = [met(ZD[i, 0, c], ZD[i, 1, c], 4) for i in range(4)]
+        rims = [first_cells(ZD[i, 0, c], ZD[i, 1, c]) for i in range(4)]
         for j in range(inner):
             for i in range(4):
                 for t in range(4):
-                    (x, y), k = ring(i, t)
-                    value = U1a[x + 2, y + 2, tile(c * inner + j), :]
-                    ZRING[4 * i + t, j * SUB:(j + 1) * SUB, :] = along_z(value, rims[i], 4 * (j * cx * cy + k), 4)
-        own = met(Z1R[0, c, 0], Z1R[1, c, 0], 4)
+                    _, k = ring(i, t)
+                    ZRING[4 * i + t, j * SUB:(j + 1) * SUB, :] += outer_z(rims[i], 4 * (j * cx * cy + k), 4)
+        own = first_cells(Z1R[0, c], Z1R[1, c])
         X, Y = (lane() >> 4) & 3, (lane() >> 2) & 3
         total = jnp.where(X == 0, roll(rims[1], -48), roll(own, 16)) + jnp.where(X == 3, roll(rims[0], 48), roll(own, -16))
         total = total + jnp.where(Y == 0, roll(rims[3], -12), roll(own, 4)) + jnp.where(Y == 3, roll(rims[2], 12), roll(own, -4))
-        total = total + Z1S[c, 0] + met(Z1R[0, c, 1], Z1R[1, c, 1], 4)
+        second_cells = jnp.where((lane() & 2) == 0, roll(Z1R[1, c], -2), Z1R[0, c])
+        total = total + ENDS[c] + second_cells
         HU[c] = own * (1.0 + third) + 0.125 * met(WZR[0], WZR[1], 4) * total
 
     def beside_xy(buffer, x, y, rows):
@@ -467,8 +490,7 @@
                 value, other = start[step, 1], start[step, 0]
                 PA[g, 9 + n] = total(value, other, near_of(step, 1, value))
 
-        @pl.loop(0, share)
-        def _(g):
+        for g in range(share):
             for n, step in enumerate(first_main):
                 w, b = main(step, share), main(step, g)
                 PB[g, n] = (w * b) * (1.0 - jacobi_weight) + w * (b + 0.03125 * PA[g, n])
@@ -490,8 +512,7 @@
             value, other = PB[g, 9], PB[g, 0]
             PA[g, 9] = total(value, other, near_of(own, 1, value))
 
-        @pl.loop(0, share)
-        def _(g):
+        for g in range(share):
             for n, step in enumerate(first_edge):
                 w, b = main(step, share), main(step, g)
                 PB[g, n] = PB[g, n] * (1.0 - jacobi_weight) + w * (b + 0.03125 * PA[g, n])
@@ -535,12 +556,17 @@
 
     @pl.loop(0, chunks)
     def _(c):
+        fine_inner(A, c)
+
+    @pl.loop(0, chunks)
+    def _(c):
         with jax.named_scope('w0'):
             fine_wait(0, c)
         with jax.named_scope('first'):
             first_pass(c)
         for copy in fine(F, 1, c):
             copy.start()
+        fine_inner(F, c)
 
     @pl.loop(0, chunks)
     def _(c):
@@ -550,6 +576,7 @@
             second_pass(c)
         for copy in one(c):
             copy.start()
+        coarse_inner(U1a, 2, c)
 
     for copy in gather_diagonal():
         copy.start()
@@ -563,12 +590,10 @@
         def _(i):
             c = h * (chunks // halves) + i
             with jax.named_scope('w2'):
-                whole(X1R.at[:, :, :, pl.ds(pl.multiple_of(c * deep, deep), deep)], one_got.at[c, 0])
-                whole(Z1R.at[:, c], one_got.at[c, 1])
-                whole(CR.at[:, c], one_got.at[c, 2])
+                whole(stage.at[pl.ds(0, 4 * (cx + cy) // 2 + 3), pl.ds(0, deep)], one_got.at[c, 0])
             with jax.named_scope('sweep'):
                 unpack_faces(c)
-                coarse_z(U1a, 2, met(Z1R[0, c, 0], Z1R[1, c, 0], 4), c)
+                coarse_outer(first_cells(Z1R[0, c], Z1R[1, c]), c)
 
                 @pl.loop(0, inner)
                 def _(j):
@@ -580,8 +605,10 @@
                             value = U1a[X + 2, Y + 2, rows, :] * third
                             U1b[X + 1, Y + 1, rows, :] = value + W1[X, Y] * (B1[k, rows, :] + 0.125 * total)
 
+                coarse_inner(U1b, 1, c)
+                ring_inner(c)
             with jax.named_scope('w3'):
-                whole(ZD.at[:, :, c], one_got.at[c, 3])
+                whole(ZD.at[:, :, c], one_got.at[c, 1])
             with jax.named_scope('ring'):
                 outside(c)
 
@@ -596,7 +623,7 @@
                             U1b[x + 1, y + 1, rows, :] = value + 0.125 * W1R[side, t] * total
 
             with jax.named_scope('residue'):
-                coarse_z(U1b, 1, HU[c], c)
+                coarse_outer(HU[c], c)
 
                 @pl.loop(0, inner)
                 def _(j):
@@ -708,14 +735,14 @@
             vmem(cx * cy, bands, nz),
             vmem(cx + 4, cy + 4, bands, nz), vmem(cx + 2, cy + 2, bands, nz), vmem(ex * ey, bands, nz),
             vmem(2, 4, cy // 2, bands, nz), vmem(2, 4, cy // 2, bands, nz),
-            vmem(chunks, 2, SUB, nz), vmem(2, chunks, 2, SUB, nz),
-            vmem(4, chunks, SUB, nz), vmem(4, chunks, SUB, nz), vmem(4, 2, chunks, SUB, nz),
+            vmem(chunks, 2, SUB, nz), vmem(2, chunks, SUB, nz),
+            vmem(4, chunks, SUB, nz), vmem(4, chunks, SUB, nz), vmem(4, 2, chunks, SUB, nz), vmem(chunks, SUB, nz),
             vmem(4, 4, SUB, nz), vmem(SUB, nz), vmem(2, SUB, nz), vmem(chunks, SUB, nz), vmem(16, deep, nz),
             vmem(2, groups // 2, SUB, nz), vmem(2, 10, groups // 2, SUB, nz), vmem(SUB, nz), vmem(10, SUB, nz),
             vmem(2, 2, SUB, nz), vmem(2, 2, SUB, nz), vmem(2, 8, 2, SUB, nz),
             vmem(9, groups // 2 + 1, SUB, nz), vmem(groups // 2, 14, SUB, nz), vmem(groups // 2, 14, SUB, nz),
             vmem(ex + 2, ey + 2, bands, nz), vmem(ex * ey, bands, nz),
-            dma(chunks), dma(3), dma(13), dma(2, chunks, 2), dma(chunks, 4), dma(2, 3), dma(3),
+            dma(chunks), dma(3), dma(13), dma(2, chunks), dma(chunks, 2), dma(2, 3), dma(3),
         ],
         compiler_params=pltpu.CompilerParams(collective_id=0, has_side_effects=True, vmem_limit_bytes=48 * 1024 * 1024),
     )(*(pltpu.with_memory_space_constraint(a, pltpu.HBM) for a in (orbitals.reshape(bands, nx * ny, nz), potential.reshape(nx * ny, nz), centre, half_width)))

time: 42.8 us -> 41.5 us (0.970)
  Pallas kernels: 41.4 us -> 40 us
    pallas_call x1, Pallas kernels: 41.4 us -> 40 us  [local(): pl.pallas_call(functools.partial(kernel, bands, nx, ny, chunks), name='fi...]
where the time goes in v6:
time: 41.5 us; the launch traced here: 41.4 us
  Pallas kernels  40 us (96%)
  local copies, waits for them, and re-layouts  1.32 us (3%)
    pallas_call x1, Pallas kernels, local(): pl.pallas_call(functools.partial(kernel, bands, nx, ny, chunks), name='fi...  40 us
    unnamed x1, local copies, waits for them, and re-layouts  1.32 us

profile of v6, /device:TPU:1, one launch (start us, length us, event | category | flops | bytes accessed | tf_op | source)
XLA Modules:
  0.0 41.4 jit_solution(506846786079671420)
XLA Ops:
  0.0 40.0 %filter_orbitals.1 = f32[64,64,128]{2,1,0:T(8,128)S(1)} custom-call(f32[64,64,128]{2,1,0:T(8,128)} %bitcast.4, f32[64,128]{1,0:T(8,128)} %bitcast.5, f32[64]{0:T(128)} %mid_hbm.1, f32[64]{0:T(128)} %half_hbm.1), custom_call_target="tpu_custom_call" | custom-call | tf_op jit(solution)/shard_map/filter_orbitals/pallas_call | solution.py:722
  40.0 1.3 %copy.6 = f32[64,8,8,128]{3,2,1,0:T(8,128)} copy(f32[64,8,8,128]{3,2,1,0:T(8,128)S(1)} %bitcast.3) | data formatting | bytes 4194304

commit v7 on v6

--- a/solution.py
+++ b/solution.py
@@ -107,7 +107,7 @@
 
 def kernel(bands, nx, ny, chunks, orb_hbm, pot_hbm, mid_hbm, half_hbm, out_ref,
            stage, pot_ref, mid_ref, half_ref, ZS, TS, A, F, S2, DG, D1, W1, MID, INV, FZS, FZR,
-           B1, U1a, U1b, B2, X1S, X1R, Z1S, Z1R, CS, CR, ZD, ENDS, W1R, WZS, WZR, HU, ZRING, MPS, MPR, WPS, WPR, EPS, EPR, XPR, XE, PA, PB, TT, TZ,
+           B1, U1a, U1b, B2, X1S, X1R, Z1S, Z1R, CS, CR, ZD, ENDS, W1S, W1R, WZS, WZR, HU, ZRING, MPS, MPR, WPS, WPR, EPS, EPR, XPR, XE, PA, PB, TT, TZ,
            in_sem, par_sem, sent, fine_got, one_got, got, got_w):
     third = 1.0 - jacobi_weight
     deep = bands // chunks
@@ -193,6 +193,12 @@
             for k in range(cx * cy):
                 total = packed(total, W1[k // cy, k % cy], 4 * (j * cx * cy + k), 4)
         WZS[...] = total
+        for d in range(4):
+            face = [W1[((cx - 1, t), (0, t), (t, cy - 1), (t, 0))[d]] for t in range(4)]
+            rows = face[0]
+            for t in range(1, 4):
+                rows = jnp.where(sublane() == t, face[t], rows)
+            W1S[d] = rows
 
     def send(src, dst, s, r, d):
         return pltpu.make_async_remote_copy(
@@ -207,7 +213,8 @@
             (FZS.at[rnd, 0, c], FZR.at[rnd, 0, c]),
             (FZS.at[rnd, 1, c], FZR.at[rnd, 1, c]),
         )
-        return [send(a, b, sent.at[d // 4], fine_got.at[rnd, c], d) for d, (a, b) in enumerate(ends)]
+        copies = [send(a, b, sent.at[d // 4], fine_got.at[rnd, c], d) for d, (a, b) in enumerate(ends)]
+        return copies[4:] + copies[:4]
 
     def whole(ref, sem):
         pltpu.make_async_copy(ref, ref, sem).wait()
@@ -345,8 +352,7 @@
                          for d in range(4)]
 
     def diagonals():
-        faces = (W1.at[cx - 1], W1.at[0], W1.at[:, cy - 1], W1.at[:, 0])
-        copies = [send(face, W1R.at[d ^ 1], sent.at[11], got_w.at[1], d) for d, face in enumerate(faces)]
+        copies = [send(W1S.at[d], W1R.at[d ^ 1], sent.at[11], got_w.at[1], d) for d in range(4)]
         return copies + [send(WZS, WZR.at[d - 4], sent.at[12], got_w.at[2], d) for d in (4, 5)]
 
     def slot(step):
@@ -442,9 +448,9 @@
         total = buffer[x - 1, y, rows, :] + buffer[x + 1, y, rows, :]
         return total + buffer[x, y - 1, rows, :] + buffer[x, y + 1, rows, :]
 
-    def level_two(h):
+    def level_two(h, early):
         at = lane()
-        for b in range(9):
+        for b in range(0 if early else 9):
             low, high = (EPR[h, 0], EPR[h, 1]) if b == 8 else (XPR[h, b, 0], XPR[h, b, 1])
             for g in range(share + 1):
                 XE[b, g] = jnp.where(at < EDGE, roll(high, -EDGE * g), roll(low, LANES - EDGE - EDGE * g))
@@ -472,7 +478,7 @@
             start = {}
             for step in first_main + RING[8:]:
                 start[step, 0] = main(step, share) * main(step, g)
-            for step in first_main:
+            for step in () if early else first_main:
                 start[step, 1] = edge(step, share) * edge(step, g)
 
             def near_of(step, part, value):
@@ -484,11 +490,20 @@
                 return near
 
             for n, step in enumerate(first_main):
-                value, other = start[step, 0], start[step, 1]
-                PA[g, n] = total(value, other, near_of(step, 0, value))
+                value = start[step, 0]
+                if early:
+                    near = near_of(step, 0, value)
+                    PA[g, n] = beside(value, near(-1, 0), near(1, 0), 2) + beside(value, near(0, -1), near(0, 1), 1)
+                else:
+                    PA[g, n] += below(value, start[step, 1]) + above(value, start[step, 1])
+            if early:
+                continue
             for n, step in enumerate(first_edge):
                 value, other = start[step, 1], start[step, 0]
                 PA[g, 9 + n] = total(value, other, near_of(step, 1, value))
+
+        if early:
+            return
 
         for g in range(share):
             for n, step in enumerate(first_main):
@@ -620,7 +635,7 @@
                             (x, y), _k = ring(side, t)
                             total = beside_xy(U1a, x + 2, y + 2, rows) + ZRING[4 * side + t, pl.ds(pl.multiple_of(j * SUB, SUB), SUB), :]
                             value = U1a[x + 2, y + 2, rows, :] * (1.0 + third)
-                            U1b[x + 1, y + 1, rows, :] = value + 0.125 * W1R[side, t] * total
+                            U1b[x + 1, y + 1, rows, :] = value + 0.125 * shape(W1R[side, t:t + 1, :]) * total
 
             with jax.named_scope('residue'):
                 coarse_outer(HU[c], c)
@@ -668,11 +683,12 @@
     def _(h):
         with jax.named_scope('w5'):
             whole(MPR.at[h], got.at[h, 0])
+        level_two(h, True)
         with jax.named_scope('w6'):
             whole(EPR.at[h], got.at[h, 1])
             whole(XPR.at[h], got.at[h, 2])
         with jax.named_scope('two'):
-            level_two(h)
+            level_two(h, False)
         with jax.named_scope('last'):
             @pl.loop(0, share)
             def _(i):
@@ -737,7 +753,7 @@
             vmem(2, 4, cy // 2, bands, nz), vmem(2, 4, cy // 2, bands, nz),
             vmem(chunks, 2, SUB, nz), vmem(2, chunks, SUB, nz),
             vmem(4, chunks, SUB, nz), vmem(4, chunks, SUB, nz), vmem(4, 2, chunks, SUB, nz), vmem(chunks, SUB, nz),
-            vmem(4, 4, SUB, nz), vmem(SUB, nz), vmem(2, SUB, nz), vmem(chunks, SUB, nz), vmem(16, deep, nz),
+            vmem(4, SUB, nz), vmem(4, SUB, nz), vmem(SUB, nz), vmem(2, SUB, nz), vmem(chunks, SUB, nz), vmem(16, deep, nz),
             vmem(2, groups // 2, SUB, nz), vmem(2, 10, groups // 2, SUB, nz), vmem(SUB, nz), vmem(10, SUB, nz),
             vmem(2, 2, SUB, nz), vmem(2, 2, SUB, nz), vmem(2, 8, 2, SUB, nz),
             vmem(9, groups // 2 + 1, SUB, nz), vmem(groups // 2, 14, SUB, nz), vmem(groups // 2, 14, SUB, nz),

time: 41.5 us -> 41 us (0.988)
  Pallas kernels: 40 us -> 39.5 us
    pallas_call x1, Pallas kernels: 40 us -> 39.5 us  [local(): pl.pallas_call(functools.partial(kernel, bands, nx, ny, chunks), name='fi...]
where the time goes in v7:
time: 41 us; the launch traced here: 40.8 us
  Pallas kernels  39.5 us (96%)
  local copies, waits for them, and re-layouts  1.32 us (3%)
    pallas_call x1, Pallas kernels, local(): pl.pallas_call(functools.partial(kernel, bands, nx, ny, chunks), name='fi...  39.5 us
    unnamed x1, local copies, waits for them, and re-layouts  1.32 us

profile of v7, /device:TPU:1, one launch (start us, length us, event | category | flops | bytes accessed | tf_op | source)
XLA Modules:
  0.0 40.8 jit_solution(2250824108261437934)
XLA Ops:
  0.0 39.5 %filter_orbitals.1 = f32[64,64,128]{2,1,0:T(8,128)S(1)} custom-call(f32[64,64,128]{2,1,0:T(8,128)} %bitcast.4, f32[64,128]{1,0:T(8,128)} %bitcast.5, f32[64]{0:T(128)} %mid_hbm.1, f32[64]{0:T(128)} %half_hbm.1), custom_call_target="tpu_custom_call" | custom-call | tf_op jit(solution)/shard_map/filter_orbitals/pallas_call | solution.py:738
  39.5 1.3 %copy.6 = f32[64,8,8,128]{3,2,1,0:T(8,128)} copy(f32[64,8,8,128]{3,2,1,0:T(8,128)S(1)} %bitcast.3) | data formatting | bytes 4194304

commit v8 on v7

--- a/solution.py
+++ b/solution.py
@@ -1,4 +1,5 @@
 import functools
+import math
 
 import jax
 import jax.numpy as jnp
@@ -343,17 +344,17 @@
         copies = []
         for i, (a, b) in enumerate(CROSS):
             for d in range(2):
-                copies.append(remote(Z1S.at[c, d], ZD.at[slot((-a, -b)), d, c], sent.at[10], one_got.at[c, 1],
+                copies.append(remote(Z1S.at[c, d], ZD.at[slot((-a, -b)), d, c], sent.at[1], one_got.at[c, 1],
                                      around_z[2 * i + d]))
-        copies += [send(Z1S.at[c, d - 4], Z1R.at[d - 4, c], sent.at[3], one_got.at[c, 0], d) for d in (4, 5)]
+        copies += [send(Z1S.at[c, d - 4], Z1R.at[d - 4, c], sent.at[1], one_got.at[c, 0], d) for d in (4, 5)]
         for i in range(4):
-            copies.append(remote(CS.at[i, c], CR.at[i, c], sent.at[9], one_got.at[c, 0], around_xy[4 + i]))
+            copies.append(remote(CS.at[i, c], CR.at[i, c], sent.at[1], one_got.at[c, 0], around_xy[4 + i]))
         return copies + [send(X1S.at[:, d, :, rows], X1R.at[:, d, :, rows], sent.at[2], one_got.at[c, 0], d)
                          for d in range(4)]
 
     def diagonals():
-        copies = [send(W1S.at[d], W1R.at[d ^ 1], sent.at[11], got_w.at[1], d) for d in range(4)]
-        return copies + [send(WZS, WZR.at[d - 4], sent.at[12], got_w.at[2], d) for d in (4, 5)]
+        copies = [send(W1S.at[d], W1R.at[d ^ 1], sent.at[1], got_w.at[1], d) for d in range(4)]
+        return copies + [send(WZS, WZR.at[d - 4], sent.at[1], got_w.at[2], d) for d in (4, 5)]
 
     def slot(step):
         return RING.index(step) if step in RING else RING.index((abs(step[0]), abs(step[1])))
@@ -365,23 +366,23 @@
     def gather(h):
         copies = []
         for i, (a, b) in enumerate(RING):
-            copies.append(remote(MPS.at[h], MPR.at[h, slot((-a, -b))], sent.at[4], got.at[h, 0], around_xy[i]))
+            copies.append(remote(MPS.at[h], MPR.at[h, slot((-a, -b))], sent.at[2], got.at[h, 0], around_xy[i]))
         return copies
 
     def gather_diagonal():
         copies = []
         for i, (a, b) in enumerate(RING):
-            copies.append(remote(WPS, WPR.at[slot((-a, -b))], sent.at[5], got_w.at[0], around_xy[i]))
+            copies.append(remote(WPS, WPR.at[slot((-a, -b))], sent.at[1], got_w.at[0], around_xy[i]))
         return copies
 
     def ends(h):
-        return [send(EPS.at[h, d], EPR.at[h, d], sent.at[6], got.at[h, 1], 4 + d) for d in range(2)]
+        return [send(EPS.at[h, d], EPR.at[h, d], sent.at[1], got.at[h, 1], 4 + d) for d in range(2)]
 
     def ends_far(h):
         copies = []
         for i, (a, b) in enumerate(NEAR):
             for d in range(2):
-                copies.append(remote(EPS.at[h, d], XPR.at[h, slot((-a, -b)), d], sent.at[7], got.at[h, 2],
+                copies.append(remote(EPS.at[h, d], XPR.at[h, slot((-a, -b)), d], sent.at[2], got.at[h, 2],
                                      around_z[2 * i + d]))
         return copies
 
@@ -677,7 +678,7 @@
 
     def store(g):
         part = pl.ds(g * SUB, SUB)
-        return pltpu.make_async_copy(stage.at[part], out_ref.at[part], sent.at[8])
+        return pltpu.make_async_copy(stage.at[part], out_ref.at[part], sent.at[3])
 
     @pl.loop(0, halves)
     def _(h):
@@ -712,19 +713,13 @@
                 store(g).start()
 
     with jax.named_scope('sent'):
+        small = (FZS, Z1R, CS, ZD, W1R, WZR, WPR, EPS)
+        large = (X1S, MPR, XPR)
+        small, large = (sum(math.prod(ref.shape) for ref in refs) // (2 * SUB * LANES) for refs in (small, large))
         whole(S2, sent.at[0])
-        whole(FZS, sent.at[1])
-        whole(X1S, sent.at[2])
-        whole(Z1R, sent.at[3])
-        whole(MPR, sent.at[4])
-        whole(WPR, sent.at[5])
-        whole(EPS, sent.at[6])
-        whole(XPR, sent.at[7])
-        whole(stage, sent.at[8])
-        whole(CS, sent.at[9])
-        whole(ZD, sent.at[10])
-        whole(W1R, sent.at[11])
-        whole(WZR, sent.at[12])
+        whole(stage.at[pl.ds(0, small), pl.ds(0, 2 * SUB)], sent.at[1])
+        whole(stage.at[pl.ds(0, large // 2), pl.ds(0, 4 * SUB)], sent.at[2])
+        whole(stage, sent.at[3])
 
 
 def local(orbitals, potential, centre, half_width):
@@ -758,7 +753,7 @@
             vmem(2, 2, SUB, nz), vmem(2, 2, SUB, nz), vmem(2, 8, 2, SUB, nz),
             vmem(9, groups // 2 + 1, SUB, nz), vmem(groups // 2, 14, SUB, nz), vmem(groups // 2, 14, SUB, nz),
             vmem(ex + 2, ey + 2, bands, nz), vmem(ex * ey, bands, nz),
-            dma(chunks), dma(3), dma(13), dma(2, chunks), dma(chunks, 2), dma(2, 3), dma(3),
+            dma(chunks), dma(3), dma(4), dma(2, chunks), dma(chunks, 2), dma(2, 3), dma(3),
         ],
         compiler_params=pltpu.CompilerParams(collective_id=0, has_side_effects=True, vmem_limit_bytes=48 * 1024 * 1024),
     )(*(pltpu.with_memory_space_constraint(a, pltpu.HBM) for a in (orbitals.reshape(bands, nx * ny, nz), potential.reshape(nx * ny, nz), centre, half_width)))

time: 41 us -> 40.9 us (level)
  no operation moved by 1% of the time
where the time goes in v8:
time: 40.9 us; the launch traced here: 40.7 us
  Pallas kernels  39.4 us (96%)
  local copies, waits for them, and re-layouts  1.32 us (3%)
    pallas_call x1, Pallas kernels, local(): pl.pallas_call(functools.partial(kernel, bands, nx, ny, chunks), name='fi...  39.4 us
    unnamed x1, local copies, waits for them, and re-layouts  1.32 us

profile of v8, /device:TPU:1, one launch (start us, length us, event | category | flops | bytes accessed | tf_op | source)
XLA Modules:
  0.0 40.7 jit_solution(2379876936208064232)
XLA Ops:
  0.0 39.4 %filter_orbitals.1 = f32[64,64,128]{2,1,0:T(8,128)S(1)} custom-call(f32[64,64,128]{2,1,0:T(8,128)} %bitcast.4, f32[64,128]{1,0:T(8,128)} %bitcast.5, f32[64]{0:T(128)} %mid_hbm.1, f32[64]{0:T(128)} %half_hbm.1), custom_call_target="tpu_custom_call" | custom-call | tf_op jit(solution)/shard_map/filter_orbitals/pallas_call | solution.py:733
  39.4 1.3 %copy.6 = f32[64,8,8,128]{3,2,1,0:T(8,128)} copy(f32[64,8,8,128]{3,2,1,0:T(8,128)S(1)} %bitcast.3) | data formatting | bytes 4194304
